TPU v7x, 256 devices: a whole 4x4x8 slice. The times are simulated.
256 devices in a mesh: ga: 32 (over y, x, z_hi), band: 8 (over z_lo, core).
Axes of the slice: x: 4, y: 4, z: 8 (z_hi: 2, z_lo: 4; z = z_hi * 4 + z_lo), core: 2. Of those that a mesh axis runs over, the one named last changes fastest.
Arguments:
- coefficients: float32 [2048, 2, 16384], P('band', None, 'ga'), may hold values from -6 to 6
- rotation: float32 [2, 2048, 256], P(None, 'band', 'ga'), may hold values from -0.1875 to 0.1875
- potential: float32 [64, 4096], P(None, 'ga'), may hold values from -2 to 0.5
- index_map: int32 [16384], replicated, may hold values from 0 to 262143, as said below
- counts: int32 [32], replicated, may hold values from 384 to 512, as said below
Outputs:
- applied_panel: float32 [256, 2, 32, 1024], P(('band', 'ga'))
Inputs may be any that keep to these rules, and one draw needn't show every extreme that they name: counts[i] counts the live slots of index i of ga, which are its slots 0 to counts[i] - 1 of 512; the counts sum to 14336, and some index has exactly 512. `index_map`: live slots name distinct cells, and together exactly 14336 cells whose signed frequency vector has a squared length no larger than that of any cell not named (a ball about the anchor), every signed component of a live cell lying in -16 to 15; dead slots name arbitrary cells.
All inputs are finite; a program needn't handle non-finite values.
Results may differ from a plain program's by a relative error of at most 0.00008.
Values sent between devices are 32-bit elements; how exact they have to be, the bound alone decides.
A program may use at most 128 MiB of HBM per device.

v0:
```python
import functools
import math

import jax
import jax.numpy as jnp
import numpy as np
from jax import lax
from jax.experimental import pallas as pl
from jax.experimental.pallas import tpu as pltpu
from jax.sharding import PartitionSpec as P

F32 = jnp.float32
BF16 = jnp.bfloat16


def split_parts(values):
    high = values.astype(BF16)
    return high, (values - high.astype(F32)).astype(BF16)


def two_parts(table):
    high = table.astype(BF16)
    low = (table - high.astype(np.float32)).astype(BF16)
    return np.stack([high, low])


def tables(box, window, radix):
    half = window // 2
    coarse = window // radix
    k_all = np.arange(box)
    k_coarse = np.arange(box // radix)
    n_signed = np.arange(window) - half
    low = np.arange(radix)
    y_phase = (radix * np.arange(coarse) - half)[:, None] * low[None, :]
    z_phase = n_signed[:, None] * k_all[None, :]
    right = y_phase[:, None, :, None] + z_phase[None, :, None, :]
    right = right.reshape(coarse * window, radix * box) % box
    x_phase = k_all[:, None] * n_signed[None, :]
    l_phase = radix * k_coarse[:, None] * low[None, :]
    left = l_phase[:, None, :, None] + x_phase[None, :, None, :]
    left = left.reshape(k_coarse.size * box, radix * window) % box
    twist = np.repeat(low[:, None] * low[None, :], box, axis=1) % box

    def pair(phase, scale=1.0):
        angle = phase * (2.0 * math.pi / box)
        return (np.stack([np.cos(angle), np.sin(angle)]) * scale).astype(np.float32)

    right_tab = two_parts(pair(right))
    left_pair = pair(left, 1.0 / box**3)
    left_tab = two_parts(left_pair)
    back_tab = two_parts((left_pair * np.float32(box**3)).transpose(0, 2, 1).copy())
    return right_tab, left_tab, back_tab, pair(twist)


def dot3(lhs, rhs, dims=((1,), (0,))):
    def one(a, b):
        return lax.dot_general(a, b, (dims, ((), ())), preferred_element_type=F32)

    return one(lhs[0], rhs[0]) + (one(lhs[0], rhs[1]) + one(lhs[1], rhs[0]))


def block(cos, sin):
    upper = jnp.concatenate([cos, sin], axis=1)
    lower = jnp.concatenate([-sin, cos], axis=1)
    return jnp.concatenate([upper, lower], axis=0)


def whole_kernel(
    bands, groups, box, window, radix, coef_hbm, rot_ref, pot_hbm, row_ref, col_ref,
    right_hbm, left_hbm, back_hbm, twist_ref, out_ref, right_ref, left_ref, back_ref, tab_sem, pot_out, acc, coef, rots, prod, land, vals,
    coef_sem, rot_send, rot_recv, pot_send, pot_recv, pass_send, pass_recv, val_send, val_recv, self_sem
):
    band = lax.axis_index("band")
    me = lax.axis_index("ga")
    total = bands * groups
    flat = band * groups + me
    cols = rot_ref.shape[1] // 2
    own = land.shape[1]
    rows = pot_hbm.shape[0] // bands
    share = pl.ds(pl.multiple_of(band * rows, rows), rows)

    loads = [
        pltpu.make_async_copy(coef_hbm.at[:, c, :], coef.at[c], coef_sem.at[c]) for c in range(2)
    ]
    for load in loads:
        load.start()
    tabs = [
        pltpu.make_async_copy(src, dst, tab_sem.at[i])
        for i, (src, dst) in enumerate(
            ((right_hbm, right_ref), (left_hbm, left_ref), (back_hbm, back_ref))
        )
    ]
    for tab in tabs:
        tab.start()
    rot_self = pltpu.make_async_copy(rot_ref.at[0], rots.at[me], self_sem.at[0])
    rot_self.start()
    pot_self = pltpu.make_async_copy(pot_hbm, pot_out.at[me], self_sem.at[1])
    pot_self.start()

    barrier = pltpu.get_barrier_semaphore()

    def greet(step, carry):
        to = lax.rem(flat + step, total)
        pl.semaphore_signal(
            barrier, inc=1, device_id={"band": to // groups, "ga": lax.rem(to, groups)},
            device_id_type=pl.DeviceIdType.MESH,
        )
        return carry

    lax.fori_loop(1, total, greet, 0)
    pl.semaphore_wait(barrier, total - 1)

    def rot_copy(to, slot):
        return pltpu.make_async_remote_copy(
            src_ref=rot_ref.at[0], dst_ref=rots.at[slot],
            send_sem=rot_send.at[to], recv_sem=rot_recv.at[slot],
            device_id={"band": band, "ga": to}, device_id_type=pl.DeviceIdType.MESH,
        )

    def pot_copy(to, slot):
        return pltpu.make_async_remote_copy(
            src_ref=pot_hbm.at[share], dst_ref=pot_out.at[slot, share],
            send_sem=pot_send.at[to], recv_sem=pot_recv.at[slot],
            device_id={"band": band, "ga": to}, device_id_type=pl.DeviceIdType.MESH,
        )

    def pass_copy(slot, to, holder):
        held = pl.ds(pl.multiple_of(holder * rows, rows), rows)
        return pltpu.make_async_remote_copy(
            src_ref=pot_out.at[slot, held], dst_ref=pot_out.at[slot, held],
            send_sem=pass_send.at[to, slot], recv_sem=pass_recv.at[holder, slot],
            device_id={"band": to, "ga": me}, device_id_type=pl.DeviceIdType.MESH,
        )

    def val_copy(to, slot):
        return pltpu.make_async_remote_copy(
            src_ref=prod.at[pl.ds(to * own, own)], dst_ref=land.at[slot],
            send_sem=val_send.at[to], recv_sem=val_recv.at[slot],
            device_id={"band": to // groups, "ga": lax.rem(to, groups)},
            device_id_type=pl.DeviceIdType.MESH,
        )

    def each(count, mine, act):
        def body(step, carry):
            act(lax.rem(mine + step, count))
            return carry

        lax.fori_loop(1, count, body, 0)

    each(groups, me, lambda to: rot_copy(to, me).start())
    each(groups, me, lambda to: pot_copy(to, me).start())
    for load in loads:
        load.wait()
    rot_self.wait()
    each(groups, me, lambda src: rot_copy(src, src).wait_recv())

    panel = groups * cols
    depth = coef.shape[1]
    real = rots[:, :cols, :].reshape(panel, depth)
    imag = rots[:, cols:, :].reshape(panel, depth)
    high, low = split_parts(jnp.concatenate([real, imag], axis=0))
    both = jnp.concatenate([high, low], axis=0)
    terms = []
    for c in range(2):
        c_high, c_low = split_parts(coef[c])
        first = jnp.dot(both, c_high, preferred_element_type=F32)
        second = jnp.dot(high, c_low, preferred_element_type=F32)
        terms.append(first[: 2 * panel] + (first[2 * panel :] + second))
    prod[:, 0, :] = terms[0][:panel] - terms[1][panel:]
    prod[:, 1, :] = terms[0][panel:] + terms[1][:panel]

    val_self = pltpu.make_async_copy(prod.at[pl.ds(flat * own, own)], land.at[flat], self_sem.at[2])
    val_self.start()
    each(total, flat, lambda to: val_copy(to, flat).start())

    def relay(src):
        pot_copy(src, src).wait_recv()
        each(bands, band, lambda to: pass_copy(src, to, band).start())

    each(groups, me, relay)
    val_self.wait()
    each(total, flat, lambda src: val_copy(src, src).wait_recv())
    summed = land[0:groups]
    for b in range(1, bands):
        summed = summed + land[b * groups : (b + 1) * groups]
    vals[...] = summed
    for tab in tabs:
        tab.wait()

    def pot_ready():
        pot_self.wait()
        each(groups, me, lambda src: each(bands, band, lambda b: pass_copy(src, b, b).wait_recv()))

    for i in range(own):
        apply_kernel(
            box, window, radix, i, pot_ready if i == 0 else None, vals, row_ref, col_ref, pot_out,
            right_ref, left_ref, back_ref, twist_ref, out_ref, acc
        )
    each(total, flat, lambda to: val_copy(to, flat).wait_send())
    each(groups, me, lambda to: rot_copy(to, me).wait_send())
    each(groups, me, lambda to: pot_copy(to, me).wait_send())
    each(groups, me, lambda src: each(bands, band, lambda b: pass_copy(src, b, band).wait_send()))


def run(coefficients, rotation, potential, row_id, col_id, consts, box, window, radix):
    bands, groups = lax.axis_size("band"), lax.axis_size("ga")
    depth, _, slots = coefficients.shape
    cols = rotation.shape[2]
    panel = cols * groups
    own = panel // (bands * groups)
    rot = rotation.transpose(0, 2, 1).reshape(1, 2 * cols, depth)
    hbm = pl.BlockSpec(memory_space=pl.ANY)
    vmem = pl.BlockSpec(memory_space=pltpu.VMEM)
    dma = pltpu.SemaphoreType.DMA
    return pl.pallas_call(
        functools.partial(whole_kernel, bands, groups, box, window, radix),
        out_shape=jax.ShapeDtypeStruct((own, 2, window, window * window), F32),
        in_specs=[hbm, vmem, hbm] + [vmem] * 2 + [hbm] * 3 + [vmem],
        out_specs=vmem,
        scratch_shapes=[
            *[pltpu.VMEM(table.shape, table.dtype) for table in consts[:3]],
            dma((3,)),
            pltpu.VMEM((groups,) + potential.shape, F32),
            pltpu.VMEM((radix * window, 4 * (window // radix) * window), F32),
            pltpu.VMEM((2, depth, slots), F32),
            pltpu.VMEM((groups, 2 * cols, depth), F32),
            pltpu.VMEM((panel, 2, slots), F32),
            pltpu.VMEM((bands * groups, own, 2, slots), F32),
            pltpu.VMEM((groups, own, 2, slots), F32),
            dma((2,)),
            dma((groups,)),
            dma((groups,)),
            dma((groups,)),
            dma((groups,)),
            dma((bands, groups)),
            dma((bands, groups)),
            dma((bands * groups,)),
            dma((bands * groups,)),
            dma((3,)),
        ],
        compiler_params=pltpu.CompilerParams(
            collective_id=0, has_side_effects=True, vmem_limit_bytes=60 * 1024 * 1024
        ),
    )(coefficients, rot, potential, row_id, col_id, *consts)


def apply_kernel(
    box, window, radix, index, pot_ready, val_ref, row_ref, col_ref, pot_ref, right_ref, left_ref, back_ref, twist_ref, out_ref, acc
):
    coarse = window // radix
    rows = radix * window
    cols = coarse * window
    wide = radix * box
    chunk = val_ref.shape[3]
    acc[...] = jnp.zeros_like(acc)

    def scatter(step, carry):
        at = pl.ds(pl.multiple_of(step * chunk, chunk), chunk)
        row_id = row_ref[:, at]
        col_id = col_ref[:, at]
        picks = lax.broadcasted_iota(jnp.int32, (rows, chunk), 0) == row_id
        onehot = jnp.where(picks, 1.0, 0.0).astype(BF16)
        hits = lax.broadcasted_iota(jnp.int32, (cols, chunk), 0) == col_id
        high, low = split_parts(val_ref[step, index])
        high, low = high.astype(F32), low.astype(F32)
        placed = [
            jnp.where(hits, part[c : c + 1, :], 0.0).astype(BF16)
            for part in (high, low)
            for c in range(2)
        ]
        acc[...] += lax.dot_general(
            onehot,
            jnp.concatenate(placed, axis=0),
            (((1,), (1,)), ((), ())),
            preferred_element_type=F32,
        )
        return carry

    lax.fori_loop(0, val_ref.shape[0], scatter, 0)
    grid_field = acc[:, : 2 * cols] + acc[:, 2 * cols :]

    right = [block(right_ref[i, 0], right_ref[i, 1]) for i in range(2)]
    field = dot3(split_parts(grid_field), right)
    cos = twist_ref[0][:, None, :]
    sin = twist_ref[1][:, None, :]
    real = field[:, :wide].reshape(radix, window, wide)
    imag = field[:, wide:].reshape(radix, window, wide)
    turned = jnp.concatenate(
        [
            (real * cos - imag * sin).reshape(rows, wide),
            (real * sin + imag * cos).reshape(rows, wide),
        ],
        axis=0,
    )
    left = [block(left_ref[i, 0], -left_ref[i, 1]) for i in range(2)]
    space = dot3(left, split_parts(turned))
    if pot_ready is not None:
        pot_ready()
    per = pot_ref.shape[0] // (box // radix)
    pot = jnp.concatenate(
        [
            jnp.concatenate([pot_ref[k * per + i] for i in range(per)], axis=1)
            for k in range(box // radix)
        ],
        axis=0,
    )
    space = space * jnp.concatenate([pot, pot], axis=0)
    back = [block(back_ref[i, 0], back_ref[i, 1]) for i in range(2)]
    field = dot3(back, split_parts(space))
    real = field[:rows].reshape(radix, window, wide)
    imag = field[rows:].reshape(radix, window, wide)
    turned = jnp.concatenate(
        [
            (real * cos + imag * sin).reshape(rows, wide),
            (imag * cos - real * sin).reshape(rows, wide),
        ],
        axis=1,
    )
    applied = dot3(split_parts(turned), right, ((1,), (1,)))

    half = window // 2
    row_at = lax.broadcasted_iota(jnp.int32, (rows, cols), 0)
    col_at = lax.broadcasted_iota(jnp.int32, (rows, cols), 1)
    n_x = (row_at % window - half).astype(F32)
    n_y = (col_at // window * radix + row_at // window - half).astype(F32)
    n_z = (col_at % window - half).astype(F32)
    kinetic = (8.0 / (box * box)) * (n_x * n_x + n_y * n_y + n_z * n_z)
    applied = applied + jnp.concatenate([kinetic, kinetic], axis=1) * grid_field
    for c in range(2):
        pieces = [
            applied[lo * window : (lo + 1) * window, c * cols + hi * window : c * cols + (hi + 1) * window]
            for hi in range(coarse)
            for lo in range(radix)
        ]
        out_ref[index, c] = jnp.concatenate(pieces, axis=1)


def per_device(coefficients, rotation, potential, index_map, counts):
    box = potential.shape[0]
    window = box // 2
    half = window // 2
    radix = math.isqrt(box)
    assert radix * radix == box
    slots_each = index_map.shape[0] // counts.shape[0]
    slot_ids = jnp.arange(slots_each, dtype=jnp.int32)
    live = (slot_ids[None, :] < counts[:, None]).reshape(-1)
    cell_x = (index_map // (box * box) + half) % box
    cell_y = (index_map // box % box + half) % box
    cell_z = (index_map % box + half) % box
    inside = (cell_x < window) & (cell_y < window) & (cell_z < window)
    row_id = jnp.where(live & inside, cell_y % radix * window + cell_x, -1)[None]
    col_id = (cell_y // radix * window + cell_z)[None]
    consts = [jnp.asarray(t) for t in tables(box, window, radix)]

    return run(coefficients, rotation, potential, row_id, col_id, consts, box, window, radix)


def solution(mesh):
    placed = (P("band", None, "ga"), P(None, "band", "ga"), P(None, "ga"), P(), P())
    return jax.shard_map(
        per_device,
        mesh=mesh,
        in_specs=placed,
        out_specs=P(("band", "ga"), None, None, None),
        check_vma=False,
    )
```

profile of v0, /device:TPU:1, one launch (start us, length us, event | category | flops | bytes accessed | tf_op | source)
XLA Modules:
  0.0 108.5 jit_solution(4368820344234155058)
XLA Ops:
  0.0 0.0 copy-start
  0.0 0.7 copy-done
  0.7 0.1 fusion.13
  0.8 1.8 %fusion.12 = (s32[16384]{0:T(1024)}, s32[16384]{0:T(1024)}) fusion(s32[16384]{0:T(1024)} %param.12, pred[16384]{0:T(1024)(128)(4,1)S(1)} %bitcast.10), kind=kLoop, calls=%fused_computation.37 | loop fusion | flops 1736704 | bytes 212992 | tf_op jit(solution)/shard_map/add | solution.py:352
  2.5 104.3 %shard_map.91 = f32[1,2,32,1024]{3,2,1,0:T(8,128)} custom-call(f32[256,2,512]{2,1,0:T(2,128)} %coef_hbm.1, f32[1,16,256]{2,1,0:T(8,128)} %bitcast.11, f32[64,128]{1,0:T(8,128)} %pot_hbm.1, s32[1,16384]{1,0:T(1,128)} %bitcast.9, s32[1,16384]{1,0:T(1,128)} %bitcast.8, bf16[2,2,128,512]{3,2,1,0:T(8,128)(2,1)} %constant.92.clone.right_hbm, ...), custom_call_target="tpu_custom_call" | custom-call | tf_op jit(solution)/shard_map/pallas_call | solution.py:215
  106.8 1.7 %copy.12 = f32[1,2,32,1024]{3,2,1,0:T(8,128)} copy(f32[1,2,32,1024]{3,2,1,0:T(8,128)} %shard_map.91) | data formatting | bytes 524288
  (1 shorter events, 0.0 us)
Async XLA Ops:
  0.0 0.7 copy-start
where the time goes:
time: 110 us; the launch traced here: 109 us
  Pallas kernels  104 us (95%)
  local copies, waits for them, and re-layouts  2.35 us (2%)
  other arithmetic  1.85 us (2%)
    pallas_call x1, Pallas kernels, run(): pl.pallas_call(functools.partial(whole_kernel, bands, groups, box, window...  104 us
    unnamed x4, local copies, waits for them, and re-layouts  2.35 us

commit v1 on v0

v1 whole, which is shorter than its diff:
```python
import functools
import math

import jax
import jax.numpy as jnp
import numpy as np
from jax import lax
from jax.experimental import pallas as pl
from jax.experimental.pallas import tpu as pltpu
from jax.sharding import PartitionSpec as P

F32 = jnp.float32
BF16 = jnp.bfloat16


def split_parts(values):
    high = values.astype(BF16)
    return high, (values - high.astype(F32)).astype(BF16)


def two_parts(table):
    high = table.astype(BF16)
    low = (table - high.astype(np.float32)).astype(BF16)
    return np.stack([high, low])


def tables(box, window, radix):
    half = window // 2
    coarse = window // radix
    k_all = np.arange(box)
    k_coarse = np.arange(box // radix)
    n_signed = np.arange(window) - half
    low = np.arange(radix)
    y_phase = (radix * np.arange(coarse) - half)[:, None] * low[None, :]
    z_phase = n_signed[:, None] * k_all[None, :]
    right = y_phase[:, None, :, None] + z_phase[None, :, None, :]
    right = right.reshape(coarse * window, radix * box) % box
    x_phase = k_all[:, None] * n_signed[None, :]
    l_phase = radix * k_coarse[:, None] * low[None, :]
    left = l_phase[:, None, :, None] + x_phase[None, :, None, :]
    left = left.reshape(k_coarse.size * box, radix * window) % box
    twist = np.repeat(low[:, None] * low[None, :], box, axis=1) % box

    def pair(phase, scale=1.0):
        angle = phase * (2.0 * math.pi / box)
        return (np.stack([np.cos(angle), np.sin(angle)]) * scale).astype(np.float32)

    right_tab = two_parts(pair(right))
    left_pair = pair(left, 1.0 / box**3)
    left_tab = two_parts(left_pair)
    back_tab = two_parts((left_pair * np.float32(box**3)).transpose(0, 2, 1).copy())
    return right_tab, left_tab, back_tab, pair(twist)


def dot3(lhs, rhs, dims=((1,), (0,))):
    def one(a, b):
        return lax.dot_general(a, b, (dims, ((), ())), preferred_element_type=F32)

    return one(lhs[0], rhs[0]) + (one(lhs[0], rhs[1]) + one(lhs[1], rhs[0]))


def block(cos, sin):
    upper = jnp.concatenate([cos, sin], axis=1)
    lower = jnp.concatenate([-sin, cos], axis=1)
    return jnp.concatenate([upper, lower], axis=0)


def whole_kernel(
    box, window, radix, coef_hbm, rot_hbm, pot_hbm, idx_hbm, cnt_hbm, right_hbm, left_hbm, back_hbm, twist_hbm,
    out_ref, coef, coef_parts, rot_own, rots, psend, drecv, ssum, zrecv, tout, land, onehot, hits, placed, acc, idx, cnt,
    pot_out, right_tab, left_tab, back_tab, twist, right_blk, left_blk, back_blk,
    load_sem, rot_send, rot_recv, pot_send, pot_recv, pair_send, pair_recv, line_send, line_recv, val_send, val_recv
):
    band = lax.axis_index("band")
    me = lax.axis_index("ga")
    groups = 2 * rots.shape[1]
    plane = groups // 2
    lines = ssum.shape[1]
    line, core = band // 2, lax.rem(band, 2)
    cell, side = me // 2, lax.rem(me, 2)
    across = cell * 2 + (1 - side)
    sibling = line * 2 + (1 - core)
    mirror = (lines - 1 - line) * 2 + core
    half_rows = pot_hbm.shape[0] // 2
    share = pl.ds(pl.multiple_of(core * half_rows, half_rows), half_rows)
    slots = coef.shape[2]

    def local(src, dst, i):
        copy = pltpu.make_async_copy(src, dst, load_sem.at[i])
        copy.start()
        return copy

    rot_load = local(rot_hbm.at[0], rot_own, 0)
    idx_load = local(idx_hbm, idx, 1)
    cnt_load = local(cnt_hbm, cnt, 2)
    coef_loads = [local(coef_hbm.at[:, c, :], coef.at[c], 3 + c) for c in range(2)]
    pot_load = local(pot_hbm, pot_out.at[me], 5)
    tab_loads = [
        local(src, dst, 6 + i)
        for i, (src, dst) in enumerate(
            ((right_hbm, right_tab), (left_hbm, left_tab), (back_hbm, back_tab), (twist_hbm, twist))
        )
    ]

    barrier = pltpu.get_barrier_semaphore()

    def greet(to_band, to):
        pl.semaphore_signal(
            barrier, inc=1, device_id={"band": to_band, "ga": to}, device_id_type=pl.DeviceIdType.MESH
        )

    def peers(act):
        def body(step, carry):
            act(lax.rem(cell + step, plane))
            return carry

        lax.fori_loop(1, plane, body, 0)

    def lines_other(act):
        for step in range(1, lines):
            act(lax.rem(line + step, lines))

    def remote(src, dst, send, recv, to_band, to):
        return pltpu.make_async_remote_copy(
            src_ref=src, dst_ref=dst, send_sem=send, recv_sem=recv,
            device_id={"band": to_band, "ga": to}, device_id_type=pl.DeviceIdType.MESH,
        )

    with jax.named_scope("barrier"):
        peers(lambda q: greet(band, q * 2 + side))
        greet(band, across)
        greet(mirror, across)
        greet(sibling, me)
        lines_other(lambda l: greet(l * 2 + core, me))
        pl.semaphore_wait(barrier, plane - 1 + 3 + lines - 1)

    def rot_swap():
        return remote(rot_own, rots.at[side, cell], rot_send.at[0], rot_recv.at[0], band, across)

    def rot_copy(which, held, q):
        slot = rots.at[held, cell]
        src = rot_own if which == 1 else slot
        return remote(src, slot, rot_send.at[which], rot_recv.at[which], band, q * 2 + side)

    def rot_all(which):
        part = rots.at[0, pl.ds(0, plane - 1)]
        return remote(part, part, rot_send.at[which], rot_recv.at[which], band, across)

    def pot_swap():
        part = pot_out.at[me, share]
        return remote(part, part, pot_send.at[0], pot_recv.at[0], mirror, across)

    def pot_copy(which, piece, q):
        part = pot_out.at[piece, share]
        return remote(part, part, pot_send.at[which], pot_recv.at[which], band, q * 2 + side)

    def pot_all(which):
        part = pot_out.at[pl.ds(0, plane - 1), pl.ds(0, half_rows)]
        return remote(part, part, pot_send.at[which], pot_recv.at[which], band, across)

    def pot_pair():
        part = pot_out.at[:, share]
        return remote(part, part, pot_send.at[3], pot_recv.at[3], sibling, me)

    def pair_copy(step):
        return remote(psend.at[step], drecv.at[step], pair_send.at[step], pair_recv.at[step], sibling, me)

    def line_copy(step, l):
        return remote(
            ssum.at[step, l], zrecv.at[step, line], line_send.at[step], line_recv.at[step], l * 2 + core, me
        )

    def line_all(step):
        part = zrecv.at[step, pl.ds(0, lines - 1)]
        return remote(part, part, line_send.at[step], line_recv.at[step], sibling, me)

    def val_copy(step, i, to):
        return remote(
            tout.at[step, i], land.at[side, cell], val_send.at[step], val_recv.at[step], band, to
        )

    def val_all(step, recv_at, count):
        part = land.at[0, pl.ds(0, count)]
        return remote(part, part, val_send.at[step], val_recv.at[recv_at], band, across)

    with jax.named_scope("send_rot"):
        rot_load.wait()
        rot_swap().start()
        peers(lambda q: rot_copy(1, side, q).start())
        rots[side, cell] = rot_own[...]
        pot_load.wait()
        pot_swap().start()

    def mark(src, carry):
        at = pl.ds(pl.multiple_of(src * slots, slots), slots)
        to = pl.ds(pl.multiple_of(src // 2 * slots, slots), slots)
        half = window // 2
        cells = idx[:, at]
        cell_x = (cells // (box * box) + half) % box
        cell_y = (cells // box % box + half) % box
        cell_z = (cells % box + half) % box
        inside = (cell_x < window) & (cell_y < window) & (cell_z < window)
        live = lax.broadcasted_iota(jnp.int32, (1, slots), 1) < cnt[src]
        row_id = jnp.where(live & inside, cell_y % radix * window + cell_x, -1)
        col_id = cell_y // radix * window + cell_z
        rows, cols = onehot.shape[1], hits.shape[1]
        picks = lax.broadcasted_iota(jnp.int32, (rows, slots), 0) == row_id
        onehot[lax.rem(src, 2), :, to] = jnp.where(picks, 1.0, 0.0).astype(BF16)
        found = lax.broadcasted_iota(jnp.int32, (cols, slots), 0) == col_id
        hits[lax.rem(src, 2), :, to] = jnp.where(found, 1.0, 0.0).astype(BF16)
        return carry

    with jax.named_scope("split_coef"):
        for c in range(2):
            coef_loads[c].wait()
            high, low = split_parts(coef[c])
            coef_parts[2 * c] = high
            coef_parts[2 * c + 1] = low
    with jax.named_scope("mark0"):
        idx_load.wait()
        cnt_load.wait()
        lax.fori_loop(0, plane // 2, mark, 0)

    with jax.named_scope("relay_rot"):
        rot_swap().wait_recv()
        peers(lambda q: rot_copy(2, 1 - side, q).start())

    def rotate(held, to_core):
        blocks = []
        for l in range(lines):
            for r in range(2):
                blocks.append(rots[held, l * 4 + to_core * 2 + r])
        a = jnp.concatenate(blocks, axis=0)
        b = jnp.concatenate(
            [piece for blk in blocks for piece in (-blk[8:], blk[:8])], axis=0
        )
        a_high, a_low = split_parts(a)
        b_high, b_low = split_parts(b)
        lhs = jnp.concatenate([a_high, a_low, a_high, b_high, b_low, b_high], axis=1)
        rhs = jnp.concatenate(
            [coef_parts[0], coef_parts[0], coef_parts[1], coef_parts[2], coef_parts[2], coef_parts[3]], axis=0
        )
        return jnp.dot(lhs, rhs, preferred_element_type=F32).reshape(lines, 2, 2, 8, slots)

    def first_part(step, held):
        with jax.named_scope(f"rotate{step}"):
            psend[step] = rotate(held, 1 - core)
            pair_copy(step).start()
            ssum[step] = rotate(held, core)

    def second_part(step):
        with jax.named_scope(f"pair{step}"):
            pair_copy(step).wait_recv()
            ssum[step] = ssum[step] + drecv[step]
            lines_other(lambda l: line_copy(step, l).start())

    def third_part(step, held):
        with jax.named_scope(f"wait_line{step}"):
            line_all(step).wait_recv()
        with jax.named_scope(f"send_val{step}"):
            total = ssum[step, line]
            for other in range(1, lines):
                total = total + zrecv[step, lax.rem(line + other, lines)]
            for r in range(2):
                for c in range(2):
                    tout[step, r * 8 : (r + 1) * 8, c, :] = total[r, c]

            def send(i, carry):
                to = i // 8 * 16 + held * 8 + lax.rem(i, 8)

                @pl.when(to != me)
                def _():
                    val_copy(step, i, to).start()

                @pl.when(to == me)
                def _():
                    land[side, cell] = tout[step, i]

                return carry

            lax.fori_loop(0, 16, send, 0)

    with jax.named_scope("wait_rot0"):
        rot_all(1).wait_recv()
    first_part(0, side)
    with jax.named_scope("relay_pot"):
        pot_swap().wait_recv()
        peers(lambda q: pot_copy(1, me, q).start())
        peers(lambda q: pot_copy(2, across, q).start())
    second_part(0)
    with jax.named_scope("wait_rot1"):
        rot_all(2).wait_recv()
    first_part(1, 1 - side)
    second_part(1)
    with jax.named_scope("mark1"):
        lax.fori_loop(plane // 2, groups, mark, 0)
    with jax.named_scope("blocks"):
        for tab in tab_loads:
            tab.wait()
        for i in range(2):
            right_blk[i] = block(right_tab[i, 0], right_tab[i, 1])
            left_blk[i] = block(left_tab[i, 0], -left_tab[i, 1])
            back_blk[i] = block(back_tab[i, 0], back_tab[i, 1])
    third_part(0, side)
    third_part(1, 1 - side)
    with jax.named_scope("pair_pot"):
        pot_all(1).wait_recv()
        pot_all(2).wait_recv()
        pot_pair().start()

    early = lax.rem(me // 8, 2)
    mine_first = early == side

    def gather(parity, alone, recv_at):
        @pl.when(alone)
        def _():
            val_all(0, recv_at, plane - 1).wait_recv()

        @pl.when(jnp.logical_not(alone))
        def _():
            val_all(0, recv_at, plane).wait_recv()

        def put(u, carry):
            to = pl.ds(pl.multiple_of(u * slots, slots), slots)
            high, low = split_parts(land[parity, u])
            mask = hits[parity, :, to]
            cols = hits.shape[1]
            for n, part in enumerate((high, low)):
                part = part.astype(F32)
                for c in range(2):
                    row = jnp.broadcast_to(part[c : c + 1, :], (16, slots)).astype(BF16)
                    full = jnp.concatenate([row] * (cols // 16), axis=0)
                    at = (2 * n + c) * cols
                    placed[at : at + cols, to] = mask * full
            return carry

        lax.fori_loop(0, plane, put, 0)
        return lax.dot_general(
            onehot[parity], placed[...], (((1,), (1,)), ((), ())), preferred_element_type=F32
        )

    acc[...] = jnp.zeros_like(acc)

    def collect(batch, carry):
        parity = lax.rem(early + batch, 2)
        with jax.named_scope("collect"):
            acc[...] += gather(parity, parity == side, batch)
        return carry

    lax.fori_loop(0, 2, collect, 0)
    cols = hits.shape[1]
    grid_field = acc[:, : 2 * cols] + acc[:, 2 * cols :]

    def pot_ready():
        pot_pair().wait_recv()

    apply_kernel(
        box, window, radix, 0, pot_ready, grid_field, pot_out, right_blk, left_blk, back_blk, twist, out_ref
    )
    with jax.named_scope("wait_sends"):
        rot_swap().wait_send()
        rot_all(1).wait_send()
        rot_all(2).wait_send()
        pot_swap().wait_send()
        pot_all(1).wait_send()
        pot_all(2).wait_send()
        pot_pair().wait_send()
        for step in range(2):
            pair_copy(step).wait_send()
            line_all(step).wait_send()
            alone = mine_first if step == 0 else jnp.logical_not(mine_first)

            @pl.when(alone)
            def _():
                val_all(step, 0, plane - 1).wait_send()

            @pl.when(jnp.logical_not(alone))
            def _():
                val_all(step, 0, plane).wait_send()


def run(coefficients, rotation, potential, index_map, counts, consts, box, window, radix):
    bands, groups = lax.axis_size("band"), lax.axis_size("ga")
    depth, _, slots = coefficients.shape
    cols = rotation.shape[2]
    assert (bands, groups, cols) == (8, 32, 8)
    lines, plane = bands // 2, groups // 2
    rot = rotation.transpose(0, 2, 1).reshape(1, 2 * cols, depth)
    hbm = pl.BlockSpec(memory_space=pl.ANY)
    vmem = pl.BlockSpec(memory_space=pltpu.VMEM)
    dma = pltpu.SemaphoreType.DMA
    rows, wide = radix * window, window // radix * window
    blocks = (2, lines, 2, 2, 8, slots)
    tabs = consts[:3]
    return pl.pallas_call(
        functools.partial(whole_kernel, box, window, radix),
        out_shape=jax.ShapeDtypeStruct((1, 2, window, window * window), F32),
        in_specs=[hbm] * 9,
        out_specs=vmem,
        scratch_shapes=[
            pltpu.VMEM((2, depth, slots), F32),
            pltpu.VMEM((4, depth, slots), BF16),
            pltpu.VMEM((2 * cols, depth), F32),
            pltpu.VMEM((2, plane, 2 * cols, depth), F32),
            pltpu.VMEM(blocks, F32),
            pltpu.VMEM(blocks, F32),
            pltpu.VMEM(blocks, F32),
            pltpu.VMEM(blocks, F32),
            pltpu.VMEM((2, 16, 2, slots), F32),
            pltpu.VMEM((2, plane, 2, slots), F32),
            pltpu.VMEM((2, rows, plane * slots), BF16),
            pltpu.VMEM((2, wide, plane * slots), BF16),
            pltpu.VMEM((4 * wide, plane * slots), BF16),
            pltpu.VMEM((rows, 4 * wide), F32),
            pltpu.VMEM((1, groups * slots), jnp.int32),
            pltpu.SMEM((groups,), jnp.int32),
            pltpu.VMEM((groups,) + potential.shape, F32),
            *[pltpu.VMEM(table.shape, table.dtype) for table in consts],
            *[pltpu.VMEM((2, 2 * table.shape[2], 2 * table.shape[3]), table.dtype) for table in tabs],
            dma((10,)),
            dma((3,)),
            dma((3,)),
            dma((4,)),
            dma((4,)),
            dma((2,)),
            dma((2,)),
            dma((2,)),
            dma((2,)),
            dma((2,)),
            dma((2,)),
        ],
        compiler_params=pltpu.CompilerParams(
            collective_id=0, has_side_effects=True, vmem_limit_bytes=60 * 1024 * 1024
        ),
    )(coefficients, rot, potential, index_map[None], counts, *consts)


def apply_kernel(
    box, window, radix, index, pot_ready, grid_field, pot_ref, right_ref, left_ref, back_ref, twist_ref, out_ref
):
    coarse = window // radix
    rows = radix * window
    cols = coarse * window
    wide = radix * box

    with jax.named_scope("fwd_fft"):
        right = [right_ref[i] for i in range(2)]
        field = dot3(split_parts(grid_field), right)
        cos = twist_ref[0][:, None, :]
        sin = twist_ref[1][:, None, :]
        real = field[:, :wide].reshape(radix, window, wide)
        imag = field[:, wide:].reshape(radix, window, wide)
        turned = jnp.concatenate(
            [
                (real * cos - imag * sin).reshape(rows, wide),
                (real * sin + imag * cos).reshape(rows, wide),
            ],
            axis=0,
        )
        left = [left_ref[i] for i in range(2)]
        space = dot3(left, split_parts(turned))
    if pot_ready is not None:
        with jax.named_scope("wait_pot"):
            pot_ready()
    per = pot_ref.shape[0] // (box // radix)
    pot = jnp.concatenate(
        [
            jnp.concatenate([pot_ref[k * per + i] for i in range(per)], axis=1)
            for k in range(box // radix)
        ],
        axis=0,
    )
    space = space * jnp.concatenate([pot, pot], axis=0)
    with jax.named_scope("back_fft"):
        back = [back_ref[i] for i in range(2)]
        field = dot3(back, split_parts(space))
        real = field[:rows].reshape(radix, window, wide)
        imag = field[rows:].reshape(radix, window, wide)
        turned = jnp.concatenate(
            [
                (real * cos + imag * sin).reshape(rows, wide),
                (imag * cos - real * sin).reshape(rows, wide),
            ],
            axis=1,
        )
        applied = dot3(split_parts(turned), right, ((1,), (1,)))

    half = window // 2
    row_at = lax.broadcasted_iota(jnp.int32, (rows, cols), 0)
    col_at = lax.broadcasted_iota(jnp.int32, (rows, cols), 1)
    n_x = (row_at % window - half).astype(F32)
    n_y = (col_at // window * radix + row_at // window - half).astype(F32)
    n_z = (col_at % window - half).astype(F32)
    kinetic = (8.0 / (box * box)) * (n_x * n_x + n_y * n_y + n_z * n_z)
    applied = applied + jnp.concatenate([kinetic, kinetic], axis=1) * grid_field
    for c in range(2):
        pieces = [
            applied[lo * window : (lo + 1) * window, c * cols + hi * window : c * cols + (hi + 1) * window]
            for hi in range(coarse)
            for lo in range(radix)
        ]
        out_ref[index, c] = jnp.concatenate(pieces, axis=1)


def per_device(coefficients, rotation, potential, index_map, counts):
    box = potential.shape[0]
    window = box // 2
    radix = math.isqrt(box)
    assert radix * radix == box
    consts = [jnp.asarray(t) for t in tables(box, window, radix)]
    return run(coefficients, rotation, potential, index_map, counts, consts, box, window, radix)


def solution(mesh):
    placed = (P("band", None, "ga"), P(None, "band", "ga"), P(None, "ga"), P(), P())
    return jax.shard_map(
        per_device,
        mesh=mesh,
        in_specs=placed,
        out_specs=P(("band", "ga"), None, None, None),
        check_vma=False,
    )
```

time: 110 us -> 51.9 us (0.47); the launches traced: 109 us -> 51.8 us
  Pallas kernels: 104 us -> 50.1 us
  other arithmetic: 1.85 us -> 0 us
    pallas_call x1, Pallas kernels: 104 us -> 50.1 us  [run(): pl.pallas_call(functools.partial(whole_kernel, box, window, radix), out_s...]
    add x1 -> x0, other arithmetic: 1.77 us -> none  [per_device(): col_id = (cell_y // radix * window + cell_z)[None]]
    unnamed x4 -> x1, local copies, waits for them, and re-layouts: 2.35 us -> 1.67 us
where the time goes in v1:
time: 51.9 us; the launch traced here: 51.8 us
  Pallas kernels  50.1 us (97%)
  local copies, waits for them, and re-layouts  1.67 us (3%)
    pallas_call x1, Pallas kernels, run(): pl.pallas_call(functools.partial(whole_kernel, box, window, radix), out_s...  50.1 us
    unnamed x1, local copies, waits for them, and re-layouts  1.67 us

profile of v1, /device:TPU:1, one launch (start us, length us, event | category | flops | bytes accessed | tf_op | source)
XLA Modules:
  0.0 51.8 jit_solution(8426202382193324495)
XLA Ops:
  0.0 50.1 %shard_map.91 = f32[1,2,32,1024]{3,2,1,0:T(8,128)} custom-call(f32[256,2,512]{2,1,0:T(2,128)} %coef_hbm.1, f32[1,16,256]{2,1,0:T(8,128)} %bitcast.5, f32[64,128]{1,0:T(8,128)} %pot_hbm.1, s32[1,16384]{1,0:T(1,128)} %bitcast.4, s32[32]{0:T(128)} %cnt_hbm.1, bf16[2,2,128,512]{3,2,1,0:T(8,128)(2,1)} %constant.8.clone.right_hbm, ...), custom_call_target="tpu_custom_call" | custom-call | tf_op jit(solution)/shard_map/pallas_call | solution.py:395
  50.1 1.7 %copy.11 = f32[1,2,32,1024]{3,2,1,0:T(8,128)} copy(f32[1,2,32,1024]{3,2,1,0:T(8,128)} %shard_map.91) | data formatting | bytes 524288

commit v2 on v1

--- a/solution.py
+++ b/solution.py
@@ -28,17 +28,13 @@
     half = window // 2
     coarse = window // radix
     k_all = np.arange(box)
-    k_coarse = np.arange(box // radix)
     n_signed = np.arange(window) - half
     low = np.arange(radix)
     y_phase = (radix * np.arange(coarse) - half)[:, None] * low[None, :]
     z_phase = n_signed[:, None] * k_all[None, :]
     right = y_phase[:, None, :, None] + z_phase[None, :, None, :]
     right = right.reshape(coarse * window, radix * box) % box
-    x_phase = k_all[:, None] * n_signed[None, :]
-    l_phase = radix * k_coarse[:, None] * low[None, :]
-    left = l_phase[:, None, :, None] + x_phase[None, :, None, :]
-    left = left.reshape(k_coarse.size * box, radix * window) % box
+    x_phase = k_all[:, None] * n_signed[None, :] % box
     twist = np.repeat(low[:, None] * low[None, :], box, axis=1) % box
 
     def pair(phase, scale=1.0):
@@ -46,10 +42,39 @@
         return (np.stack([np.cos(angle), np.sin(angle)]) * scale).astype(np.float32)
 
     right_tab = two_parts(pair(right))
-    left_pair = pair(left, 1.0 / box**3)
-    left_tab = two_parts(left_pair)
-    back_tab = two_parts((left_pair * np.float32(box**3)).transpose(0, 2, 1).copy())
+    cos, sin = pair(x_phase)
+    left_high, left_low = two_parts(np.block([[cos, -sin], [sin, cos]]) / np.float32(box**3))
+    left_tab = np.concatenate([left_high, left_low, left_high, left_low], axis=1)
+    back_high, back_low = two_parts(np.block([[cos.T, sin.T], [-sin.T, cos.T]]))
+    back_tab = np.block([[back_high, back_high], [back_low, back_low]])
     return right_tab, left_tab, back_tab, pair(twist)
+
+
+def fft8(values, sign):
+    root = math.sqrt(0.5)
+
+    def add(a, b):
+        return a[0] + b[0], a[1] + b[1]
+
+    def sub(a, b):
+        return a[0] - b[0], a[1] - b[1]
+
+    def turn(a):
+        return (-a[1], a[0]) if sign > 0 else (a[1], -a[0])
+
+    def fft4(a, b, c, d):
+        total, diff = add(a, c), sub(a, c)
+        other, cross = add(b, d), turn(sub(b, d))
+        return add(total, other), add(diff, cross), sub(total, other), sub(diff, cross)
+
+    even = fft4(*values[0::2])
+    odd = list(fft4(*values[1::2]))
+    one, three = odd[1], odd[3]
+    one_turn, three_turn = turn(one), turn(three)
+    odd[1] = ((one[0] + one_turn[0]) * root, (one[1] + one_turn[1]) * root)
+    odd[2] = turn(odd[2])
+    odd[3] = ((three_turn[0] - three[0]) * root, (three_turn[1] - three[1]) * root)
+    return [add(a, b) for a, b in zip(even, odd)] + [sub(a, b) for a, b in zip(even, odd)]
 
 
 def dot3(lhs, rhs, dims=((1,), (0,))):
@@ -68,7 +93,7 @@
 def whole_kernel(
     box, window, radix, coef_hbm, rot_hbm, pot_hbm, idx_hbm, cnt_hbm, right_hbm, left_hbm, back_hbm, twist_hbm,
     out_ref, coef, coef_parts, rot_own, rots, psend, drecv, ssum, zrecv, tout, land, onehot, hits, placed, acc, idx, cnt,
-    pot_out, right_tab, left_tab, back_tab, twist, right_blk, left_blk, back_blk,
+    pot_out, right_tab, left_tab, back_tab, twist, right_blk, field, mixed, unmixed, turned,
     load_sem, rot_send, rot_recv, pot_send, pot_recv, pair_send, pair_recv, line_send, line_recv, val_send, val_recv
 ):
     band = lax.axis_index("band")
@@ -176,12 +201,12 @@
 
     def val_copy(step, i, to):
         return remote(
-            tout.at[step, i], land.at[side, cell], val_send.at[step], val_recv.at[step], band, to
-        )
-
-    def val_all(step, recv_at, count):
+            tout.at[step, i], land.at[side, cell], val_send.at[step], val_recv.at[step, cell // 4], band, to
+        )
+
+    def val_all(step, batch, row, count):
         part = land.at[0, pl.ds(0, count)]
-        return remote(part, part, val_send.at[step], val_recv.at[recv_at], band, across)
+        return remote(part, part, val_send.at[step], val_recv.at[batch, row], band, across)
 
     with jax.named_scope("send_rot"):
         rot_load.wait()
@@ -299,8 +324,6 @@
             tab.wait()
         for i in range(2):
             right_blk[i] = block(right_tab[i, 0], right_tab[i, 1])
-            left_blk[i] = block(left_tab[i, 0], -left_tab[i, 1])
-            back_blk[i] = block(back_tab[i, 0], back_tab[i, 1])
     third_part(0, side)
     third_part(1, 1 - side)
     with jax.named_scope("pair_pot"):
@@ -310,44 +333,43 @@
 
     early = lax.rem(me // 8, 2)
     mine_first = early == side
-
-    def gather(parity, alone, recv_at):
+    acc[...] = jnp.zeros_like(acc)
+
+    def collect(step, carry):
+        batch, near = step // 4, lax.rem(step, 4)
+        parity = lax.rem(early + batch, 2)
+        row = lax.rem(cell // 4 + near + near // 2 - 2 * (near // 3), 4)
+        alone = (parity == side) & (row == cell // 4)
+
         @pl.when(alone)
         def _():
-            val_all(0, recv_at, plane - 1).wait_recv()
+            val_all(0, batch, row, 3).wait_recv()
 
         @pl.when(jnp.logical_not(alone))
         def _():
-            val_all(0, recv_at, plane).wait_recv()
-
-        def put(u, carry):
-            to = pl.ds(pl.multiple_of(u * slots, slots), slots)
-            high, low = split_parts(land[parity, u])
+            val_all(0, batch, row, 4).wait_recv()
+
+        deep = 4 * slots
+        span = pl.ds(pl.multiple_of(row * deep, deep), deep)
+        cols = hits.shape[1]
+        for u in range(4):
+            to = pl.ds(pl.multiple_of(row * deep + u * slots, slots), slots)
+            high, low = split_parts(land[parity, row * 4 + u])
             mask = hits[parity, :, to]
-            cols = hits.shape[1]
             for n, part in enumerate((high, low)):
                 part = part.astype(F32)
                 for c in range(2):
-                    row = jnp.broadcast_to(part[c : c + 1, :], (16, slots)).astype(BF16)
-                    full = jnp.concatenate([row] * (cols // 16), axis=0)
+                    line_of = jnp.broadcast_to(part[c : c + 1, :], (16, slots)).astype(BF16)
+                    full = jnp.concatenate([line_of] * (cols // 16), axis=0)
                     at = (2 * n + c) * cols
-                    placed[at : at + cols, to] = mask * full
-            return carry
-
-        lax.fori_loop(0, plane, put, 0)
-        return lax.dot_general(
-            onehot[parity], placed[...], (((1,), (1,)), ((), ())), preferred_element_type=F32
-        )
-
-    acc[...] = jnp.zeros_like(acc)
-
-    def collect(batch, carry):
-        parity = lax.rem(early + batch, 2)
-        with jax.named_scope("collect"):
-            acc[...] += gather(parity, parity == side, batch)
+                    placed[at : at + cols, u * slots : (u + 1) * slots] = mask * full
+        acc[...] += lax.dot_general(
+            onehot[parity, :, span], placed[...], (((1,), (1,)), ((), ())), preferred_element_type=F32
+        )
         return carry
 
-    lax.fori_loop(0, 2, collect, 0)
+    with jax.named_scope("collect"):
+        lax.fori_loop(0, 8, collect, 0)
     cols = hits.shape[1]
     grid_field = acc[:, : 2 * cols] + acc[:, 2 * cols :]
 
@@ -355,7 +377,8 @@
         pot_pair().wait_recv()
 
     apply_kernel(
-        box, window, radix, 0, pot_ready, grid_field, pot_out, right_blk, left_blk, back_blk, twist, out_ref
+        box, window, radix, pot_ready, grid_field, pot_out, right_blk, left_tab, back_tab, twist,
+        field, mixed, unmixed, turned, out_ref
     )
     with jax.named_scope("wait_sends"):
         rot_swap().wait_send()
@@ -372,11 +395,11 @@
 
             @pl.when(alone)
             def _():
-                val_all(step, 0, plane - 1).wait_send()
+                val_all(step, 0, 0, plane - 1).wait_send()
 
             @pl.when(jnp.logical_not(alone))
             def _():
-                val_all(step, 0, plane).wait_send()
+                val_all(step, 0, 0, plane).wait_send()
 
 
 def run(coefficients, rotation, potential, index_map, counts, consts, box, window, radix):
@@ -391,7 +414,6 @@
     dma = pltpu.SemaphoreType.DMA
     rows, wide = radix * window, window // radix * window
     blocks = (2, lines, 2, 2, 8, slots)
-    tabs = consts[:3]
     return pl.pallas_call(
         functools.partial(whole_kernel, box, window, radix),
         out_shape=jax.ShapeDtypeStruct((1, 2, window, window * window), F32),
@@ -410,13 +432,17 @@
             pltpu.VMEM((2, plane, 2, slots), F32),
             pltpu.VMEM((2, rows, plane * slots), BF16),
             pltpu.VMEM((2, wide, plane * slots), BF16),
-            pltpu.VMEM((4 * wide, plane * slots), BF16),
+            pltpu.VMEM((4 * wide, 4 * slots), BF16),
             pltpu.VMEM((rows, 4 * wide), F32),
             pltpu.VMEM((1, groups * slots), jnp.int32),
             pltpu.SMEM((groups,), jnp.int32),
             pltpu.VMEM((groups,) + potential.shape, F32),
             *[pltpu.VMEM(table.shape, table.dtype) for table in consts],
-            *[pltpu.VMEM((2, 2 * table.shape[2], 2 * table.shape[3]), table.dtype) for table in tabs],
+            pltpu.VMEM((2, 2 * wide, 2 * radix * box), BF16),
+            pltpu.VMEM((rows, 2 * radix * box), F32),
+            pltpu.VMEM((2, radix, 2 * window, radix * box), BF16),
+            pltpu.VMEM((radix, 2 * window, radix * box), F32),
+            pltpu.VMEM((2, rows, 2 * radix * box), BF16),
             dma((10,)),
             dma((3,)),
             dma((3,)),
@@ -427,7 +453,7 @@
             dma((2,)),
             dma((2,)),
             dma((2,)),
-            dma((2,)),
+            dma((2, 4)),
         ],
         compiler_params=pltpu.CompilerParams(
             collective_id=0, has_side_effects=True, vmem_limit_bytes=60 * 1024 * 1024
@@ -436,54 +462,70 @@
 
 
 def apply_kernel(
-    box, window, radix, index, pot_ready, grid_field, pot_ref, right_ref, left_ref, back_ref, twist_ref, out_ref
+    box, window, radix, pot_ready, grid_field, pot_ref, right_ref, left_ref, back_ref, twist_ref,
+    field_ref, mixed_ref, unmixed_ref, turned_ref, out_ref
 ):
     coarse = window // radix
     rows = radix * window
     cols = coarse * window
     wide = radix * box
-
-    with jax.named_scope("fwd_fft"):
+    lanes = 128
+    per = wide // pot_ref.shape[2]
+
+    with jax.named_scope("fwd_right"):
         right = [right_ref[i] for i in range(2)]
-        field = dot3(split_parts(grid_field), right)
-        cos = twist_ref[0][:, None, :]
-        sin = twist_ref[1][:, None, :]
-        real = field[:, :wide].reshape(radix, window, wide)
-        imag = field[:, wide:].reshape(radix, window, wide)
-        turned = jnp.concatenate(
-            [
-                (real * cos - imag * sin).reshape(rows, wide),
-                (real * sin + imag * cos).reshape(rows, wide),
-            ],
-            axis=0,
-        )
-        left = [left_ref[i] for i in range(2)]
-        space = dot3(left, split_parts(turned))
-    if pot_ready is not None:
-        with jax.named_scope("wait_pot"):
-            pot_ready()
-    per = pot_ref.shape[0] // (box // radix)
-    pot = jnp.concatenate(
-        [
-            jnp.concatenate([pot_ref[k * per + i] for i in range(per)], axis=1)
-            for k in range(box // radix)
-        ],
-        axis=0,
-    )
-    space = space * jnp.concatenate([pot, pot], axis=0)
-    with jax.named_scope("back_fft"):
-        back = [back_ref[i] for i in range(2)]
-        field = dot3(back, split_parts(space))
-        real = field[:rows].reshape(radix, window, wide)
-        imag = field[rows:].reshape(radix, window, wide)
-        turned = jnp.concatenate(
-            [
-                (real * cos + imag * sin).reshape(rows, wide),
-                (imag * cos - real * sin).reshape(rows, wide),
-            ],
-            axis=1,
-        )
-        applied = dot3(split_parts(turned), right, ((1,), (1,)))
+        field_ref[...] = dot3(split_parts(grid_field), right)
+
+    def mix(tile, carry):
+        at = pl.ds(pl.multiple_of(tile * lanes, lanes), lanes)
+        imag_at = pl.ds(pl.multiple_of(wide + tile * lanes, lanes), lanes)
+        values = []
+        for low in range(radix):
+            real = field_ref[low * window : (low + 1) * window, at]
+            imag = field_ref[low * window : (low + 1) * window, imag_at]
+            cos, sin = twist_ref[0, low : low + 1, at], twist_ref[1, low : low + 1, at]
+            values.append((real * cos - imag * sin, real * sin + imag * cos))
+        for k, pair in enumerate(fft8(values, 1)):
+            for c in range(2):
+                high, low = split_parts(pair[c])
+                mixed_ref[0, k, c * window : (c + 1) * window, at] = high
+                mixed_ref[1, k, c * window : (c + 1) * window, at] = low
+        return carry
+
+    with jax.named_scope("mix"):
+        lax.fori_loop(0, wide // lanes, mix, 0)
+    with jax.named_scope("wait_pot"):
+        pot_ready()
+
+    with jax.named_scope("left"):
+        for k in range(radix):
+            high, low = mixed_ref[0, k], mixed_ref[1, k]
+            space = jnp.dot(
+                left_ref[...], jnp.concatenate([high, high, low, low], axis=0), preferred_element_type=F32
+            )
+            pot = jnp.concatenate([pot_ref[k * per + i] for i in range(per)], axis=1)
+            high, low = split_parts(space * jnp.concatenate([pot, pot], axis=0))
+            both = jnp.dot(back_ref[...], jnp.concatenate([high, low], axis=0), preferred_element_type=F32)
+            unmixed_ref[k] = both[: 2 * window] + both[2 * window :]
+
+    def unmix(tile, carry):
+        at = pl.ds(pl.multiple_of(tile * lanes, lanes), lanes)
+        imag_at = pl.ds(pl.multiple_of(wide + tile * lanes, lanes), lanes)
+        values = [
+            (unmixed_ref[k, :window, at], unmixed_ref[k, window:, at]) for k in range(radix)
+        ]
+        for low, (real, imag) in enumerate(fft8(values, -1)):
+            cos, sin = twist_ref[0, low : low + 1, at], twist_ref[1, low : low + 1, at]
+            turned = (real * cos + imag * sin, imag * cos - real * sin)
+            for value, to in zip(turned, (at, imag_at)):
+                for i, part in enumerate(split_parts(value)):
+                    turned_ref[i, low * window : (low + 1) * window, to] = part
+        return carry
+
+    with jax.named_scope("unmix"):
+        lax.fori_loop(0, wide // lanes, unmix, 0)
+    with jax.named_scope("back_right"):
+        applied = dot3([turned_ref[0], turned_ref[1]], right, ((1,), (1,)))
 
     half = window // 2
     row_at = lax.broadcasted_iota(jnp.int32, (rows, cols), 0)
@@ -499,7 +541,7 @@
             for hi in range(coarse)
             for lo in range(radix)
         ]
-        out_ref[index, c] = jnp.concatenate(pieces, axis=1)
+        out_ref[0, c] = jnp.concatenate(pieces, axis=1)
 
 
 def per_device(coefficients, rotation, potential, index_map, counts):

time: 51.9 us -> 49.5 us (0.954)
  Pallas kernels: 50.1 us -> 47.8 us
    pallas_call x1, Pallas kernels: 50.1 us -> 47.8 us  [run(): pl.pallas_call(functools.partial(whole_kernel, box, window, radix), out_s...]
where the time goes in v2:
time: 49.5 us; the launch traced here: 49.4 us
  Pallas kernels  47.8 us (97%)
  local copies, waits for them, and re-layouts  1.67 us (3%)
    pallas_call x1, Pallas kernels, run(): pl.pallas_call(functools.partial(whole_kernel, box, window, radix), out_s...  47.8 us
    unnamed x1, local copies, waits for them, and re-layouts  1.67 us

profile of v2, /device:TPU:1, one launch (start us, length us, event | category | flops | bytes accessed | tf_op | source)
XLA Modules:
  0.0 49.4 jit_solution(1758004017478726357)
XLA Ops:
  0.0 47.8 %shard_map.91 = f32[1,2,32,1024]{3,2,1,0:T(8,128)} custom-call(f32[256,2,512]{2,1,0:T(2,128)} %coef_hbm.1, f32[1,16,256]{2,1,0:T(8,128)} %bitcast.5, f32[64,128]{1,0:T(8,128)} %pot_hbm.1, s32[1,16384]{1,0:T(1,128)} %bitcast.4, s32[32]{0:T(128)} %cnt_hbm.1, bf16[2,2,128,512]{3,2,1,0:T(8,128)(2,1)} %constant.8.clone.right_hbm, ...), custom_call_target="tpu_custom_call" | custom-call | tf_op jit(solution)/shard_map/pallas_call | solution.py:417
  47.8 1.7 %copy.11 = f32[1,2,32,1024]{3,2,1,0:T(8,128)} copy(f32[1,2,32,1024]{3,2,1,0:T(8,128)} %shard_map.91) | data formatting | bytes 524288

commit v3 on v2

--- a/solution.py
+++ b/solution.py
@@ -92,7 +92,7 @@
 
 def whole_kernel(
     box, window, radix, coef_hbm, rot_hbm, pot_hbm, idx_hbm, cnt_hbm, right_hbm, left_hbm, back_hbm, twist_hbm,
-    out_ref, coef, coef_parts, rot_own, rots, psend, drecv, ssum, zrecv, tout, land, onehot, hits, placed, acc, idx, cnt,
+    out_ref, coef, coef_parts, rot_raw, rot_own, rots, psend, drecv, ssum, zrecv, tout, land, onehot, hits, placed, acc, idx, cnt,
     pot_out, right_tab, left_tab, back_tab, twist, right_blk, field, mixed, unmixed, turned,
     load_sem, rot_send, rot_recv, pot_send, pot_recv, pair_send, pair_recv, line_send, line_recv, val_send, val_recv
 ):
@@ -115,7 +115,7 @@
         copy.start()
         return copy
 
-    rot_load = local(rot_hbm.at[0], rot_own, 0)
+    rot_load = local(rot_hbm.at[0], rot_raw, 0)
     idx_load = local(idx_hbm, idx, 1)
     cnt_load = local(cnt_hbm, cnt, 2)
     coef_loads = [local(coef_hbm.at[:, c, :], coef.at[c], 3 + c) for c in range(2)]
@@ -135,21 +135,40 @@
         )
 
     def peers(act):
-        def body(step, carry):
-            act(lax.rem(cell + step, plane))
-            return carry
-
-        lax.fori_loop(1, plane, body, 0)
+        def body(step, code):
+            shift = lax.rem(code, 16)
+            act(lax.rem(cell // 4 + shift // 4, 4) * 4 + lax.rem(cell + shift, 4))
+            return code // 16
+
+        lax.fori_loop(0, 8, body, jnp.int32(0x528E6B9A))
+        lax.fori_loop(0, 7, body, jnp.int32(0xC431FD7))
 
     def lines_other(act):
-        for step in range(1, lines):
-            act(lax.rem(line + step, lines))
+        low = 1 - line // 2
+        for step in range(lines):
+            l = low * (lines - 1 - step) + (1 - low) * step
+
+            @pl.when(l != line)
+            def _(l=l):
+                act(l)
 
     def remote(src, dst, send, recv, to_band, to):
         return pltpu.make_async_remote_copy(
             src_ref=src, dst_ref=dst, send_sem=send, recv_sem=recv,
             device_id={"band": to_band, "ga": to}, device_id_type=pl.DeviceIdType.MESH,
         )
+
+    def split_coef():
+        for c in range(2):
+            coef_loads[c].wait()
+            high, low = split_parts(coef[c])
+            coef_parts[2 * c] = high
+            coef_parts[2 * c + 1] = low
+        rot_load.wait()
+        for e in range(2):
+            for c in range(2):
+                for x in range(4):
+                    rot_own[e, 4 * c + x] = rot_raw[8 * c + 2 * x + e]
 
     with jax.named_scope("barrier"):
         peers(lambda q: greet(band, q * 2 + side))
@@ -157,6 +176,7 @@
         greet(mirror, across)
         greet(sibling, me)
         lines_other(lambda l: greet(l * 2 + core, me))
+        split_coef()
         pl.semaphore_wait(barrier, plane - 1 + 3 + lines - 1)
 
     def rot_swap():
@@ -199,9 +219,9 @@
         part = zrecv.at[step, pl.ds(0, lines - 1)]
         return remote(part, part, line_send.at[step], line_recv.at[step], sibling, me)
 
-    def val_copy(step, i, to):
+    def val_copy(step, i, to_band, to):
         return remote(
-            tout.at[step, i], land.at[side, cell], val_send.at[step], val_recv.at[step, cell // 4], band, to
+            tout.at[step, i], land.at[side, cell], val_send.at[step], val_recv.at[step, cell // 4], to_band, to
         )
 
     def val_all(step, batch, row, count):
@@ -209,7 +229,6 @@
         return remote(part, part, val_send.at[step], val_recv.at[batch, row], band, across)
 
     with jax.named_scope("send_rot"):
-        rot_load.wait()
         rot_swap().start()
         peers(lambda q: rot_copy(1, side, q).start())
         rots[side, cell] = rot_own[...]
@@ -235,30 +254,24 @@
         hits[lax.rem(src, 2), :, to] = jnp.where(found, 1.0, 0.0).astype(BF16)
         return carry
 
-    with jax.named_scope("split_coef"):
-        for c in range(2):
-            coef_loads[c].wait()
-            high, low = split_parts(coef[c])
-            coef_parts[2 * c] = high
-            coef_parts[2 * c + 1] = low
     with jax.named_scope("mark0"):
         idx_load.wait()
         cnt_load.wait()
-        lax.fori_loop(0, plane // 2, mark, 0)
+        lax.fori_loop(0, 4, mark, 0)
 
     with jax.named_scope("relay_rot"):
         rot_swap().wait_recv()
         peers(lambda q: rot_copy(2, 1 - side, q).start())
+        lax.fori_loop(4, 8, mark, 0)
 
     def rotate(held, to_core):
         blocks = []
         for l in range(lines):
-            for r in range(2):
-                blocks.append(rots[held, l * 4 + to_core * 2 + r])
+            for l_of, e in ((l, side), (lines - 1 - l, 1 - side)):
+                for r in range(2):
+                    blocks.append(rots[held, l_of * 4 + to_core * 2 + r, e])
         a = jnp.concatenate(blocks, axis=0)
-        b = jnp.concatenate(
-            [piece for blk in blocks for piece in (-blk[8:], blk[:8])], axis=0
-        )
+        b = jnp.concatenate([piece for blk in blocks for piece in (-blk[4:], blk[:4])], axis=0)
         a_high, a_low = split_parts(a)
         b_high, b_low = split_parts(b)
         lhs = jnp.concatenate([a_high, a_low, a_high, b_high, b_low, b_high], axis=1)
@@ -286,16 +299,23 @@
             total = ssum[step, line]
             for other in range(1, lines):
                 total = total + zrecv[step, lax.rem(line + other, lines)]
-            for r in range(2):
-                for c in range(2):
-                    tout[step, r * 8 : (r + 1) * 8, c, :] = total[r, c]
-
-            def send(i, carry):
-                to = i // 8 * 16 + held * 8 + lax.rem(i, 8)
+            for e in range(2):
+                for r in range(2):
+                    for c in range(2):
+                        at = e * 8 + r * 4
+                        tout[step, at : at + 4, c, :] = total[e, r, c * 4 : c * 4 + 4]
+
+            def send(n, carry):
+                e = 1 - n // 8
+                r = lax.rem(cell // 8 + 1 + n // 4, 2)
+                m = lax.rem(n, 4)
+                x = lax.rem(cell + jnp.where(m == 0, 2, jnp.where(m == 1, 1, jnp.where(m == 2, 3, 0))), 4)
+                to = (r * 8 + held * 4 + x) * 2 + lax.rem(side + e, 2)
+                i = e * 8 + r * 4 + x
 
                 @pl.when(to != me)
                 def _():
-                    val_copy(step, i, to).start()
+                    val_copy(step, i, (1 - e) * band + e * mirror, to).start()
 
                 @pl.when(to == me)
                 def _():
@@ -318,18 +338,19 @@
     first_part(1, 1 - side)
     second_part(1)
     with jax.named_scope("mark1"):
-        lax.fori_loop(plane // 2, groups, mark, 0)
-    with jax.named_scope("blocks"):
+        lax.fori_loop(8, 16, mark, 0)
         for tab in tab_loads:
             tab.wait()
         for i in range(2):
             right_blk[i] = block(right_tab[i, 0], right_tab[i, 1])
-    third_part(0, side)
-    third_part(1, 1 - side)
     with jax.named_scope("pair_pot"):
         pot_all(1).wait_recv()
         pot_all(2).wait_recv()
         pot_pair().start()
+    third_part(0, side)
+    with jax.named_scope("mark2"):
+        lax.fori_loop(16, groups, mark, 0)
+    third_part(1, 1 - side)
 
     early = lax.rem(me // 8, 2)
     mine_first = early == side
@@ -423,7 +444,8 @@
             pltpu.VMEM((2, depth, slots), F32),
             pltpu.VMEM((4, depth, slots), BF16),
             pltpu.VMEM((2 * cols, depth), F32),
-            pltpu.VMEM((2, plane, 2 * cols, depth), F32),
+            pltpu.VMEM((2, cols, depth), F32),
+            pltpu.VMEM((2, plane, 2, cols, depth), F32),
             pltpu.VMEM(blocks, F32),
             pltpu.VMEM(blocks, F32),
             pltpu.VMEM(blocks, F32),

time: 49.5 us -> 46.8 us (0.945)
  Pallas kernels: 47.8 us -> 45 us
    pallas_call x1, Pallas kernels: 47.8 us -> 45 us  [run(): pl.pallas_call(functools.partial(whole_kernel, box, window, radix), out_s...]
where the time goes in v3:
time: 46.8 us; the launch traced here: 46.6 us
  Pallas kernels  45 us (96%)
  local copies, waits for them, and re-layouts  1.67 us (4%)
    pallas_call x1, Pallas kernels, run(): pl.pallas_call(functools.partial(whole_kernel, box, window, radix), out_s...  45 us
    unnamed x1, local copies, waits for them, and re-layouts  1.67 us

profile of v3, /device:TPU:1, one launch (start us, length us, event | category | flops | bytes accessed | tf_op | source)
XLA Modules:
  0.0 46.6 jit_solution(17440656355939862952)
XLA Ops:
  0.0 45.0 %shard_map.91 = f32[1,2,32,1024]{3,2,1,0:T(8,128)} custom-call(f32[256,2,512]{2,1,0:T(2,128)} %coef_hbm.1, f32[1,16,256]{2,1,0:T(8,128)} %bitcast.5, f32[64,128]{1,0:T(8,128)} %pot_hbm.1, s32[1,16384]{1,0:T(1,128)} %bitcast.4, s32[32]{0:T(128)} %cnt_hbm.1, bf16[2,2,128,512]{3,2,1,0:T(8,128)(2,1)} %constant.8.clone.right_hbm, ...), custom_call_target="tpu_custom_call" | custom-call | tf_op jit(solution)/shard_map/pallas_call | solution.py:438
  45.0 1.7 %copy.11 = f32[1,2,32,1024]{3,2,1,0:T(8,128)} copy(f32[1,2,32,1024]{3,2,1,0:T(8,128)} %shard_map.91) | data formatting | bytes 524288

commit v4 on v3

--- a/solution.py
+++ b/solution.py
@@ -92,7 +92,7 @@
 
 def whole_kernel(
     box, window, radix, coef_hbm, rot_hbm, pot_hbm, idx_hbm, cnt_hbm, right_hbm, left_hbm, back_hbm, twist_hbm,
-    out_ref, coef, coef_parts, rot_raw, rot_own, rots, psend, drecv, ssum, zrecv, tout, land, onehot, hits, placed, acc, idx, cnt,
+    out_ref, coef, coef_parts, rot_raw, rot_own, rots, prod, drecv, zrecv, tout, land, onehot, hits, placed, acc, idx, cnt,
     pot_out, right_tab, left_tab, back_tab, twist, right_blk, field, mixed, unmixed, turned,
     load_sem, rot_send, rot_recv, pot_send, pot_recv, pair_send, pair_recv, line_send, line_recv, val_send, val_recv
 ):
@@ -100,7 +100,7 @@
     me = lax.axis_index("ga")
     groups = 2 * rots.shape[1]
     plane = groups // 2
-    lines = ssum.shape[1]
+    lines = zrecv.shape[1]
     line, core = band // 2, lax.rem(band, 2)
     cell, side = me // 2, lax.rem(me, 2)
     across = cell * 2 + (1 - side)
@@ -208,11 +208,11 @@
         return remote(part, part, pot_send.at[3], pot_recv.at[3], sibling, me)
 
     def pair_copy(step):
-        return remote(psend.at[step], drecv.at[step], pair_send.at[step], pair_recv.at[step], sibling, me)
+        return remote(prod.at[step, 0], drecv.at[step], pair_send.at[step], pair_recv.at[step], sibling, me)
 
     def line_copy(step, l):
         return remote(
-            ssum.at[step, l], zrecv.at[step, line], line_send.at[step], line_recv.at[step], l * 2 + core, me
+            prod.at[step, 1, l], zrecv.at[step, line], line_send.at[step], line_recv.at[step], l * 2 + core, me
         )
 
     def line_all(step):
@@ -230,10 +230,10 @@
 
     with jax.named_scope("send_rot"):
         rot_swap().start()
+        pot_load.wait()
+        pot_swap().start()
         peers(lambda q: rot_copy(1, side, q).start())
         rots[side, cell] = rot_own[...]
-        pot_load.wait()
-        pot_swap().start()
 
     def mark(src, carry):
         at = pl.ds(pl.multiple_of(src * slots, slots), slots)
@@ -261,6 +261,7 @@
 
     with jax.named_scope("relay_rot"):
         rot_swap().wait_recv()
+        pot_swap().wait_recv()
         peers(lambda q: rot_copy(2, 1 - side, q).start())
         lax.fori_loop(4, 8, mark, 0)
 
@@ -280,23 +281,48 @@
         )
         return jnp.dot(lhs, rhs, preferred_element_type=F32).reshape(lines, 2, 2, 8, slots)
 
-    def first_part(step, held):
-        with jax.named_scope(f"rotate{step}"):
-            psend[step] = rotate(held, 1 - core)
-            pair_copy(step).start()
-            ssum[step] = rotate(held, core)
-
-    def second_part(step):
-        with jax.named_scope(f"pair{step}"):
+    def first_half(step, carry):
+        with jax.named_scope("wait_rot"):
+            rot_all(1 + step).wait_recv()
+
+        def part(i, carry):
+            with jax.named_scope("rotate"):
+                prod[step, i] = rotate(lax.rem(side + step, 2), lax.rem(core + 1 + i, 2))
+
+            @pl.when(i == 0)
+            def _():
+                pair_copy(step).start()
+
+            return carry
+
+        lax.fori_loop(0, 2, part, 0)
+
+        @pl.when(step == 1)
+        def _():
+            with jax.named_scope("relay_pot"):
+                peers(lambda q: pot_copy(1, me, q).start())
+                peers(lambda q: pot_copy(2, across, q).start())
+
+        with jax.named_scope("pair"):
             pair_copy(step).wait_recv()
-            ssum[step] = ssum[step] + drecv[step]
+            prod[step, 1] = prod[step, 1] + drecv[step]
             lines_other(lambda l: line_copy(step, l).start())
-
-    def third_part(step, held):
-        with jax.named_scope(f"wait_line{step}"):
+        return carry
+
+    lax.fori_loop(0, 2, first_half, 0)
+    with jax.named_scope("blocks"):
+        for tab in tab_loads:
+            tab.wait()
+        for i in range(2):
+            right_blk[i] = block(right_tab[i, 0], right_tab[i, 1])
+
+    def second_half(step, carry):
+        with jax.named_scope("mark1"):
+            lax.fori_loop(8 + 12 * step, 20 + 12 * step, mark, 0)
+        with jax.named_scope("wait_line"):
             line_all(step).wait_recv()
-        with jax.named_scope(f"send_val{step}"):
-            total = ssum[step, line]
+        with jax.named_scope("send_val"):
+            total = prod[step, 1, line]
             for other in range(1, lines):
                 total = total + zrecv[step, lax.rem(line + other, lines)]
             for e in range(2):
@@ -310,7 +336,7 @@
                 r = lax.rem(cell // 8 + 1 + n // 4, 2)
                 m = lax.rem(n, 4)
                 x = lax.rem(cell + jnp.where(m == 0, 2, jnp.where(m == 1, 1, jnp.where(m == 2, 3, 0))), 4)
-                to = (r * 8 + held * 4 + x) * 2 + lax.rem(side + e, 2)
+                to = (r * 8 + lax.rem(side + step, 2) * 4 + x) * 2 + lax.rem(side + e, 2)
                 i = e * 8 + r * 4 + x
 
                 @pl.when(to != me)
@@ -324,33 +350,13 @@
                 return carry
 
             lax.fori_loop(0, 16, send, 0)
-
-    with jax.named_scope("wait_rot0"):
-        rot_all(1).wait_recv()
-    first_part(0, side)
-    with jax.named_scope("relay_pot"):
-        pot_swap().wait_recv()
-        peers(lambda q: pot_copy(1, me, q).start())
-        peers(lambda q: pot_copy(2, across, q).start())
-    second_part(0)
-    with jax.named_scope("wait_rot1"):
-        rot_all(2).wait_recv()
-    first_part(1, 1 - side)
-    second_part(1)
-    with jax.named_scope("mark1"):
-        lax.fori_loop(8, 16, mark, 0)
-        for tab in tab_loads:
-            tab.wait()
-        for i in range(2):
-            right_blk[i] = block(right_tab[i, 0], right_tab[i, 1])
+        return carry
+
+    lax.fori_loop(0, 2, second_half, 0)
     with jax.named_scope("pair_pot"):
         pot_all(1).wait_recv()
         pot_all(2).wait_recv()
         pot_pair().start()
-    third_part(0, side)
-    with jax.named_scope("mark2"):
-        lax.fori_loop(16, groups, mark, 0)
-    third_part(1, 1 - side)
 
     early = lax.rem(me // 8, 2)
     mine_first = early == side
@@ -446,8 +452,7 @@
             pltpu.VMEM((2 * cols, depth), F32),
             pltpu.VMEM((2, cols, depth), F32),
             pltpu.VMEM((2, plane, 2, cols, depth), F32),
-            pltpu.VMEM(blocks, F32),
-            pltpu.VMEM(blocks, F32),
+            pltpu.VMEM((2,) + blocks, F32),
             pltpu.VMEM(blocks, F32),
             pltpu.VMEM(blocks, F32),
             pltpu.VMEM((2, 16, 2, slots), F32),
@@ -495,8 +500,14 @@
     per = wide // pot_ref.shape[2]
 
     with jax.named_scope("fwd_right"):
-        right = [right_ref[i] for i in range(2)]
-        field_ref[...] = dot3(split_parts(grid_field), right)
+        parts = split_parts(grid_field)
+
+        def spread(c, carry):
+            at = pl.ds(pl.multiple_of(c * wide, wide), wide)
+            field_ref[:, at] = dot3(parts, [right_ref[i, :, at] for i in range(2)])
+            return carry
+
+        lax.fori_loop(0, 2, spread, 0)
 
     def mix(tile, carry):
         at = pl.ds(pl.multiple_of(tile * lanes, lanes), lanes)
@@ -521,14 +532,16 @@
 
     with jax.named_scope("left"):
         for k in range(radix):
-            high, low = mixed_ref[0, k], mixed_ref[1, k]
-            space = jnp.dot(
-                left_ref[...], jnp.concatenate([high, high, low, low], axis=0), preferred_element_type=F32
-            )
-            pot = jnp.concatenate([pot_ref[k * per + i] for i in range(per)], axis=1)
-            high, low = split_parts(space * jnp.concatenate([pot, pot], axis=0))
-            both = jnp.dot(back_ref[...], jnp.concatenate([high, low], axis=0), preferred_element_type=F32)
-            unmixed_ref[k] = both[: 2 * window] + both[2 * window :]
+            for n in range(2):
+                at = slice(n * 2 * lanes, (n + 1) * 2 * lanes)
+                high, low = mixed_ref[0, k, :, at], mixed_ref[1, k, :, at]
+                space = jnp.dot(
+                    left_ref[...], jnp.concatenate([high, high, low, low], axis=0), preferred_element_type=F32
+                )
+                pot = jnp.concatenate([pot_ref[k * per + 2 * n + i] for i in range(2)], axis=1)
+                high, low = split_parts(space * jnp.concatenate([pot, pot], axis=0))
+                both = jnp.dot(back_ref[...], jnp.concatenate([high, low], axis=0), preferred_element_type=F32)
+                unmixed_ref[k, :, at] = both[: 2 * window] + both[2 * window :]
 
     def unmix(tile, carry):
         at = pl.ds(pl.multiple_of(tile * lanes, lanes), lanes)
@@ -547,7 +560,7 @@
     with jax.named_scope("unmix"):
         lax.fori_loop(0, wide // lanes, unmix, 0)
     with jax.named_scope("back_right"):
-        applied = dot3([turned_ref[0], turned_ref[1]], right, ((1,), (1,)))
+        applied = dot3([turned_ref[0], turned_ref[1]], [right_ref[0], right_ref[1]], ((1,), (1,)))
 
     half = window // 2
     row_at = lax.broadcasted_iota(jnp.int32, (rows, cols), 0)

time: 46.8 us -> 44.5 us (0.951)
  Pallas kernels: 45 us -> 42.7 us
    pallas_call x1, Pallas kernels: 45 us -> 42.7 us  [run(): pl.pallas_call(functools.partial(whole_kernel, box, window, radix), out_s...]
where the time goes in v4:
time: 44.5 us; the launch traced here: 44.4 us
  Pallas kernels  42.7 us (96%)
  local copies, waits for them, and re-layouts  1.67 us (4%)
    pallas_call x1, Pallas kernels, run(): pl.pallas_call(functools.partial(whole_kernel, box, window, radix), out_s...  42.7 us
    unnamed x1, local copies, waits for them, and re-layouts  1.67 us

profile of v4, /device:TPU:1, one launch (start us, length us, event | category | flops | bytes accessed | tf_op | source)
XLA Modules:
  0.0 44.4 jit_solution(17204951632955934795)
XLA Ops:
  0.0 42.7 %shard_map.91 = f32[1,2,32,1024]{3,2,1,0:T(8,128)} custom-call(f32[256,2,512]{2,1,0:T(2,128)} %coef_hbm.1, f32[1,16,256]{2,1,0:T(8,128)} %bitcast.5, f32[64,128]{1,0:T(8,128)} %pot_hbm.1, s32[1,16384]{1,0:T(1,128)} %bitcast.4, s32[32]{0:T(128)} %cnt_hbm.1, bf16[2,2,128,512]{3,2,1,0:T(8,128)(2,1)} %constant.8.clone.right_hbm, ...), custom_call_target="tpu_custom_call" | custom-call | tf_op jit(solution)/shard_map/pallas_call | solution.py:444
  42.7 1.7 %copy.11 = f32[1,2,32,1024]{3,2,1,0:T(8,128)} copy(f32[1,2,32,1024]{3,2,1,0:T(8,128)} %shard_map.91) | data formatting | bytes 524288

commit v5 on v4

--- a/solution.py
+++ b/solution.py
@@ -92,9 +92,10 @@
 
 def whole_kernel(
     box, window, radix, coef_hbm, rot_hbm, pot_hbm, idx_hbm, cnt_hbm, right_hbm, left_hbm, back_hbm, twist_hbm,
-    out_ref, coef, coef_parts, rot_raw, rot_own, rots, prod, drecv, zrecv, tout, land, onehot, hits, placed, acc, idx, cnt,
-    pot_out, right_tab, left_tab, back_tab, twist, right_blk, field, mixed, unmixed, turned,
-    load_sem, rot_send, rot_recv, pot_send, pot_recv, pair_send, pair_recv, line_send, line_recv, val_send, val_recv
+    out_ref, coef, coef_parts, rot_raw, rot_own, rots, prod, drecv, zrecv, tout, land, onehot, hits, acc, idx, cnt,
+    pot_out, right_tab, left_tab, back_tab, twist, right_blk, field, mixed, unmixed, turned, kinetic, out_buf,
+    load_sem, rot_send, rot_recv, pot_send, pot_recv, pair_send, pair_recv, line_send, line_recv, val_send, val_recv,
+    out_sem
 ):
     band = lax.axis_index("band")
     me = lax.axis_index("ga")
@@ -115,6 +116,44 @@
         copy.start()
         return copy
 
+    barrier = pltpu.get_barrier_semaphore()
+
+    def greet(to_band, to):
+        pl.semaphore_signal(
+            barrier, inc=1, device_id={"band": to_band, "ga": to}, device_id_type=pl.DeviceIdType.MESH
+        )
+
+    def peers(act):
+        def body(step, code):
+            shift = lax.rem(code, 16)
+            act(lax.rem(cell // 4 + shift // 4, 4) * 4 + lax.rem(cell + shift, 4))
+            return code // 16
+
+        lax.fori_loop(0, 8, body, jnp.int32(0x528E6B9A))
+        lax.fori_loop(0, 7, body, jnp.int32(0xC431FD7))
+
+    def lines_other(act):
+        low = 1 - line // 2
+        for step in range(lines):
+            l = low * (lines - 1 - step) + (1 - low) * step
+
+            @pl.when(l != line)
+            def _(l=l):
+                act(l)
+
+    def remote(src, dst, send, recv, to_band, to):
+        return pltpu.make_async_remote_copy(
+            src_ref=src, dst_ref=dst, send_sem=send, recv_sem=recv,
+            device_id={"band": to_band, "ga": to}, device_id_type=pl.DeviceIdType.MESH,
+        )
+
+    with jax.named_scope("barrier"):
+        greet(band, across)
+        greet(mirror, across)
+        peers(lambda q: greet(band, q * 2 + side))
+        lines_other(lambda l: greet(l * 2 + core, me))
+        greet(sibling, me)
+
     rot_load = local(rot_hbm.at[0], rot_raw, 0)
     idx_load = local(idx_hbm, idx, 1)
     cnt_load = local(cnt_hbm, cnt, 2)
@@ -127,37 +166,6 @@
         )
     ]
 
-    barrier = pltpu.get_barrier_semaphore()
-
-    def greet(to_band, to):
-        pl.semaphore_signal(
-            barrier, inc=1, device_id={"band": to_band, "ga": to}, device_id_type=pl.DeviceIdType.MESH
-        )
-
-    def peers(act):
-        def body(step, code):
-            shift = lax.rem(code, 16)
-            act(lax.rem(cell // 4 + shift // 4, 4) * 4 + lax.rem(cell + shift, 4))
-            return code // 16
-
-        lax.fori_loop(0, 8, body, jnp.int32(0x528E6B9A))
-        lax.fori_loop(0, 7, body, jnp.int32(0xC431FD7))
-
-    def lines_other(act):
-        low = 1 - line // 2
-        for step in range(lines):
-            l = low * (lines - 1 - step) + (1 - low) * step
-
-            @pl.when(l != line)
-            def _(l=l):
-                act(l)
-
-    def remote(src, dst, send, recv, to_band, to):
-        return pltpu.make_async_remote_copy(
-            src_ref=src, dst_ref=dst, send_sem=send, recv_sem=recv,
-            device_id={"band": to_band, "ga": to}, device_id_type=pl.DeviceIdType.MESH,
-        )
-
     def split_coef():
         for c in range(2):
             coef_loads[c].wait()
@@ -170,12 +178,7 @@
                 for x in range(4):
                     rot_own[e, 4 * c + x] = rot_raw[8 * c + 2 * x + e]
 
-    with jax.named_scope("barrier"):
-        peers(lambda q: greet(band, q * 2 + side))
-        greet(band, across)
-        greet(mirror, across)
-        greet(sibling, me)
-        lines_other(lambda l: greet(l * 2 + core, me))
+    with jax.named_scope("barrier_wait"):
         split_coef()
         pl.semaphore_wait(barrier, plane - 1 + 3 + lines - 1)
 
@@ -210,18 +213,19 @@
     def pair_copy(step):
         return remote(prod.at[step, 0], drecv.at[step], pair_send.at[step], pair_recv.at[step], sibling, me)
 
-    def line_copy(step, l):
+    def line_copy(step, e, l):
         return remote(
-            prod.at[step, 1, l], zrecv.at[step, line], line_send.at[step], line_recv.at[step], l * 2 + core, me
+            prod.at[step, 1, l, e], zrecv.at[step, line, e], line_send.at[step, e], line_recv.at[step, e],
+            l * 2 + core, me,
         )
 
-    def line_all(step):
-        part = zrecv.at[step, pl.ds(0, lines - 1)]
-        return remote(part, part, line_send.at[step], line_recv.at[step], sibling, me)
-
-    def val_copy(step, i, to_band, to):
+    def line_all(step, e):
+        part = zrecv.at[step, pl.ds(0, lines - 1), 0]
+        return remote(part, part, line_send.at[step, e], line_recv.at[step, e], sibling, me)
+
+    def val_copy(step, turn, i, to_band, to):
         return remote(
-            tout.at[step, i], land.at[side, cell], val_send.at[step], val_recv.at[step, cell // 4], to_band, to
+            tout.at[turn, i], land.at[side, cell], val_send.at[step], val_recv.at[step, cell // 4], to_band, to
         )
 
     def val_all(step, batch, row, count):
@@ -297,16 +301,18 @@
 
         lax.fori_loop(0, 2, part, 0)
 
+        with jax.named_scope("pair"):
+            pair_copy(step).wait_recv()
+            prod[step, 1] = prod[step, 1] + drecv[step]
+            for e in (1, 0):
+                lines_other(lambda l: line_copy(step, e, l).start())
+
         @pl.when(step == 1)
         def _():
             with jax.named_scope("relay_pot"):
                 peers(lambda q: pot_copy(1, me, q).start())
                 peers(lambda q: pot_copy(2, across, q).start())
 
-        with jax.named_scope("pair"):
-            pair_copy(step).wait_recv()
-            prod[step, 1] = prod[step, 1] + drecv[step]
-            lines_other(lambda l: line_copy(step, l).start())
         return carry
 
     lax.fori_loop(0, 2, first_half, 0)
@@ -315,44 +321,44 @@
             tab.wait()
         for i in range(2):
             right_blk[i] = block(right_tab[i, 0], right_tab[i, 1])
-
-    def second_half(step, carry):
+        kinetic[...] = kinetic_factors(box, window, radix)
+
+    def second_half(turn, carry):
+        step, e = turn // 2, 1 - lax.rem(turn, 2)
         with jax.named_scope("mark1"):
-            lax.fori_loop(8 + 12 * step, 20 + 12 * step, mark, 0)
+            before = jnp.where(turn == 0, 8, jnp.where(turn == 1, 20, jnp.where(turn == 2, 30, groups)))
+            lax.fori_loop(jnp.where(turn == 0, 8, jnp.where(turn == 1, 8, jnp.where(turn == 2, 20, 30))), before, mark, 0)
         with jax.named_scope("wait_line"):
-            line_all(step).wait_recv()
+            line_all(step, e).wait_recv()
         with jax.named_scope("send_val"):
-            total = prod[step, 1, line]
+            total = prod[step, 1, line, e]
             for other in range(1, lines):
-                total = total + zrecv[step, lax.rem(line + other, lines)]
-            for e in range(2):
-                for r in range(2):
-                    for c in range(2):
-                        at = e * 8 + r * 4
-                        tout[step, at : at + 4, c, :] = total[e, r, c * 4 : c * 4 + 4]
+                total = total + zrecv[step, lax.rem(line + other, lines), e]
+            for r in range(2):
+                for c in range(2):
+                    tout[turn, r * 4 : r * 4 + 4, c, :] = total[r, c * 4 : c * 4 + 4]
 
             def send(n, carry):
-                e = 1 - n // 8
                 r = lax.rem(cell // 8 + 1 + n // 4, 2)
                 m = lax.rem(n, 4)
                 x = lax.rem(cell + jnp.where(m == 0, 2, jnp.where(m == 1, 1, jnp.where(m == 2, 3, 0))), 4)
                 to = (r * 8 + lax.rem(side + step, 2) * 4 + x) * 2 + lax.rem(side + e, 2)
-                i = e * 8 + r * 4 + x
+                i = r * 4 + x
 
                 @pl.when(to != me)
                 def _():
-                    val_copy(step, i, (1 - e) * band + e * mirror, to).start()
+                    val_copy(step, turn, i, (1 - e) * band + e * mirror, to).start()
 
                 @pl.when(to == me)
                 def _():
-                    land[side, cell] = tout[step, i]
+                    land[side, cell] = tout[turn, i]
 
                 return carry
 
-            lax.fori_loop(0, 16, send, 0)
+            lax.fori_loop(0, 8, send, 0)
         return carry
 
-    lax.fori_loop(0, 2, second_half, 0)
+    lax.fori_loop(0, 4, second_half, 0)
     with jax.named_scope("pair_pot"):
         pot_all(1).wait_recv()
         pot_all(2).wait_recv()
@@ -379,35 +385,44 @@
         deep = 4 * slots
         span = pl.ds(pl.multiple_of(row * deep, deep), deep)
         cols = hits.shape[1]
+        placed = [[], []]
         for u in range(4):
             to = pl.ds(pl.multiple_of(row * deep + u * slots, slots), slots)
-            high, low = split_parts(land[parity, row * 4 + u])
             mask = hits[parity, :, to]
-            for n, part in enumerate((high, low)):
+            for n, part in enumerate(split_parts(land[parity, row * 4 + u])):
                 part = part.astype(F32)
+                pieces = []
                 for c in range(2):
                     line_of = jnp.broadcast_to(part[c : c + 1, :], (16, slots)).astype(BF16)
-                    full = jnp.concatenate([line_of] * (cols // 16), axis=0)
-                    at = (2 * n + c) * cols
-                    placed[at : at + cols, u * slots : (u + 1) * slots] = mask * full
-        acc[...] += lax.dot_general(
-            onehot[parity, :, span], placed[...], (((1,), (1,)), ((), ())), preferred_element_type=F32
+                    pieces.append(mask * jnp.concatenate([line_of] * (cols // 16), axis=0))
+                placed[n].append(jnp.concatenate(pieces, axis=0))
+        picked = onehot[parity, :, span]
+        high, low = (
+            lax.dot_general(
+                picked, jnp.concatenate(part, axis=1), (((1,), (1,)), ((), ())), preferred_element_type=F32
+            )
+            for part in placed
         )
+        acc[...] += high + low
         return carry
 
     with jax.named_scope("collect"):
         lax.fori_loop(0, 8, collect, 0)
-    cols = hits.shape[1]
-    grid_field = acc[:, : 2 * cols] + acc[:, 2 * cols :]
+    grid_field = acc[...]
 
     def pot_ready():
         pot_pair().wait_recv()
 
+    def out_copy(c):
+        return pltpu.make_async_copy(out_buf.at[c], out_ref.at[0, c], out_sem.at[c])
+
     apply_kernel(
-        box, window, radix, pot_ready, grid_field, pot_out, right_blk, left_tab, back_tab, twist,
-        field, mixed, unmixed, turned, out_ref
+        box, window, radix, band >= 0, pot_ready, grid_field, pot_out, right_blk, left_tab, back_tab, twist,
+        field, mixed, unmixed, turned, kinetic, out_buf, lambda c: out_copy(c).start()
     )
     with jax.named_scope("wait_sends"):
+        for c in range(2):
+            out_copy(c).wait()
         rot_swap().wait_send()
         rot_all(1).wait_send()
         rot_all(2).wait_send()
@@ -417,7 +432,8 @@
         pot_pair().wait_send()
         for step in range(2):
             pair_copy(step).wait_send()
-            line_all(step).wait_send()
+            for e in range(2):
+                line_all(step, e).wait_send()
             alone = mine_first if step == 0 else jnp.logical_not(mine_first)
 
             @pl.when(alone)
@@ -437,7 +453,6 @@
     lines, plane = bands // 2, groups // 2
     rot = rotation.transpose(0, 2, 1).reshape(1, 2 * cols, depth)
     hbm = pl.BlockSpec(memory_space=pl.ANY)
-    vmem = pl.BlockSpec(memory_space=pltpu.VMEM)
     dma = pltpu.SemaphoreType.DMA
     rows, wide = radix * window, window // radix * window
     blocks = (2, lines, 2, 2, 8, slots)
@@ -445,7 +460,7 @@
         functools.partial(whole_kernel, box, window, radix),
         out_shape=jax.ShapeDtypeStruct((1, 2, window, window * window), F32),
         in_specs=[hbm] * 9,
-        out_specs=vmem,
+        out_specs=hbm,
         scratch_shapes=[
             pltpu.VMEM((2, depth, slots), F32),
             pltpu.VMEM((4, depth, slots), BF16),
@@ -455,12 +470,11 @@
             pltpu.VMEM((2,) + blocks, F32),
             pltpu.VMEM(blocks, F32),
             pltpu.VMEM(blocks, F32),
-            pltpu.VMEM((2, 16, 2, slots), F32),
+            pltpu.VMEM((4, 8, 2, slots), F32),
             pltpu.VMEM((2, plane, 2, slots), F32),
             pltpu.VMEM((2, rows, plane * slots), BF16),
             pltpu.VMEM((2, wide, plane * slots), BF16),
-            pltpu.VMEM((4 * wide, 4 * slots), BF16),
-            pltpu.VMEM((rows, 4 * wide), F32),
+            pltpu.VMEM((rows, 2 * wide), F32),
             pltpu.VMEM((1, groups * slots), jnp.int32),
             pltpu.SMEM((groups,), jnp.int32),
             pltpu.VMEM((groups,) + potential.shape, F32),
@@ -470,6 +484,8 @@
             pltpu.VMEM((2, radix, 2 * window, radix * box), BF16),
             pltpu.VMEM((radix, 2 * window, radix * box), F32),
             pltpu.VMEM((2, rows, 2 * radix * box), BF16),
+            pltpu.VMEM((rows, wide), F32),
+            pltpu.VMEM((2, window, window * window), F32),
             dma((10,)),
             dma((3,)),
             dma((3,)),
@@ -477,10 +493,11 @@
             dma((4,)),
             dma((2,)),
             dma((2,)),
-            dma((2,)),
-            dma((2,)),
+            dma((2, 2)),
+            dma((2, 2)),
             dma((2,)),
             dma((2, 4)),
+            dma((2,)),
         ],
         compiler_params=pltpu.CompilerParams(
             collective_id=0, has_side_effects=True, vmem_limit_bytes=60 * 1024 * 1024
@@ -488,9 +505,20 @@
     )(coefficients, rot, potential, index_map[None], counts, *consts)
 
 
+def kinetic_factors(box, window, radix):
+    rows, cols = radix * window, window // radix * window
+    half = window // 2
+    row_at = lax.broadcasted_iota(jnp.int32, (rows, cols), 0)
+    col_at = lax.broadcasted_iota(jnp.int32, (rows, cols), 1)
+    n_x = (row_at % window - half).astype(F32)
+    n_y = (col_at // window * radix + row_at // window - half).astype(F32)
+    n_z = (col_at % window - half).astype(F32)
+    return (8.0 / (box * box)) * (n_x * n_x + n_y * n_y + n_z * n_z)
+
+
 def apply_kernel(
-    box, window, radix, pot_ready, grid_field, pot_ref, right_ref, left_ref, back_ref, twist_ref,
-    field_ref, mixed_ref, unmixed_ref, turned_ref, out_ref
+    box, window, radix, apart, pot_ready, grid_field, pot_ref, right_ref, left_ref, back_ref, twist_ref,
+    field_ref, mixed_ref, unmixed_ref, turned_ref, kinetic_ref, out_ref, ship
 ):
     coarse = window // radix
     rows = radix * window
@@ -500,14 +528,7 @@
     per = wide // pot_ref.shape[2]
 
     with jax.named_scope("fwd_right"):
-        parts = split_parts(grid_field)
-
-        def spread(c, carry):
-            at = pl.ds(pl.multiple_of(c * wide, wide), wide)
-            field_ref[:, at] = dot3(parts, [right_ref[i, :, at] for i in range(2)])
-            return carry
-
-        lax.fori_loop(0, 2, spread, 0)
+        field_ref[...] = dot3(split_parts(grid_field), [right_ref[0], right_ref[1]])
 
     def mix(tile, carry):
         at = pl.ds(pl.multiple_of(tile * lanes, lanes), lanes)
@@ -531,17 +552,19 @@
         pot_ready()
 
     with jax.named_scope("left"):
-        for k in range(radix):
-            for n in range(2):
-                at = slice(n * 2 * lanes, (n + 1) * 2 * lanes)
-                high, low = mixed_ref[0, k, :, at], mixed_ref[1, k, :, at]
-                space = jnp.dot(
-                    left_ref[...], jnp.concatenate([high, high, low, low], axis=0), preferred_element_type=F32
-                )
-                pot = jnp.concatenate([pot_ref[k * per + 2 * n + i] for i in range(2)], axis=1)
-                high, low = split_parts(space * jnp.concatenate([pot, pot], axis=0))
-                both = jnp.dot(back_ref[...], jnp.concatenate([high, low], axis=0), preferred_element_type=F32)
-                unmixed_ref[k, :, at] = both[: 2 * window] + both[2 * window :]
+        @pl.when(apart)
+        def _():
+            for k in range(radix):
+                for n in range(2):
+                    at = slice(n * 2 * lanes, (n + 1) * 2 * lanes)
+                    high, low = mixed_ref[0, k, :, at], mixed_ref[1, k, :, at]
+                    space = jnp.dot(
+                        left_ref[...], jnp.concatenate([high, high, low, low], axis=0), preferred_element_type=F32
+                    )
+                    pot = jnp.concatenate([pot_ref[k * per + 2 * n + i] for i in range(2)], axis=1)
+                    high, low = split_parts(space * jnp.concatenate([pot, pot], axis=0))
+                    both = jnp.dot(back_ref[...], jnp.concatenate([high, low], axis=0), preferred_element_type=F32)
+                    unmixed_ref[k, :, at] = both[: 2 * window] + both[2 * window :]
 
     def unmix(tile, carry):
         at = pl.ds(pl.multiple_of(tile * lanes, lanes), lanes)
@@ -562,13 +585,7 @@
     with jax.named_scope("back_right"):
         applied = dot3([turned_ref[0], turned_ref[1]], [right_ref[0], right_ref[1]], ((1,), (1,)))
 
-    half = window // 2
-    row_at = lax.broadcasted_iota(jnp.int32, (rows, cols), 0)
-    col_at = lax.broadcasted_iota(jnp.int32, (rows, cols), 1)
-    n_x = (row_at % window - half).astype(F32)
-    n_y = (col_at // window * radix + row_at // window - half).astype(F32)
-    n_z = (col_at % window - half).astype(F32)
-    kinetic = (8.0 / (box * box)) * (n_x * n_x + n_y * n_y + n_z * n_z)
+    kinetic = kinetic_ref[...]
     applied = applied + jnp.concatenate([kinetic, kinetic], axis=1) * grid_field
     for c in range(2):
         pieces = [
@@ -576,7 +593,8 @@
             for hi in range(coarse)
             for lo in range(radix)
         ]
-        out_ref[0, c] = jnp.concatenate(pieces, axis=1)
+        out_ref[c] = jnp.concatenate(pieces, axis=1)
+        ship(c)
 
 
 def per_device(coefficients, rotation, potential, index_map, counts):

time: 44.5 us -> 44.1 us (level)
  Pallas kernels: 42.7 us -> 42.2 us
    pallas_call x1, Pallas kernels: 42.7 us -> 42.2 us  [run(): pl.pallas_call(functools.partial(whole_kernel, box, window, radix), out_s...]
where the time goes in v5:
time: 44.1 us; the launch traced here: 43.9 us
  Pallas kernels  42.2 us (96%)
  local copies, waits for them, and re-layouts  1.67 us (4%)
    pallas_call x1, Pallas kernels, run(): pl.pallas_call(functools.partial(whole_kernel, box, window, radix), out_s...  42.2 us
    unnamed x1, local copies, waits for them, and re-layouts  1.67 us

profile of v5, /device:TPU:1, one launch (start us, length us, event | category | flops | bytes accessed | tf_op | source)
XLA Modules:
  0.0 43.9 jit_solution(14943622071482969956)
XLA Ops:
  0.0 42.2 %shard_map.91 = f32[1,2,32,1024]{3,2,1,0:T(8,128)} custom-call(f32[256,2,512]{2,1,0:T(2,128)} %coef_hbm.1, f32[1,16,256]{2,1,0:T(8,128)} %bitcast.5, f32[64,128]{1,0:T(8,128)} %pot_hbm.1, s32[1,16384]{1,0:T(1,128)} %bitcast.4, s32[32]{0:T(128)} %cnt_hbm.1, bf16[2,2,128,512]{3,2,1,0:T(8,128)(2,1)} %constant.8.clone.right_hbm, ...), custom_call_target="tpu_custom_call" | custom-call | tf_op jit(solution)/shard_map/pallas_call | solution.py:459
  42.3 1.7 %copy.11 = f32[1,2,32,1024]{3,2,1,0:T(8,128)} copy(f32[1,2,32,1024]{3,2,1,0:T(8,128)} %shard_map.91) | data formatting | bytes 524288

commit v6 on v5

--- a/solution.py
+++ b/solution.py
@@ -322,47 +322,6 @@
         for i in range(2):
             right_blk[i] = block(right_tab[i, 0], right_tab[i, 1])
         kinetic[...] = kinetic_factors(box, window, radix)
-
-    def second_half(turn, carry):
-        step, e = turn // 2, 1 - lax.rem(turn, 2)
-        with jax.named_scope("mark1"):
-            before = jnp.where(turn == 0, 8, jnp.where(turn == 1, 20, jnp.where(turn == 2, 30, groups)))
-            lax.fori_loop(jnp.where(turn == 0, 8, jnp.where(turn == 1, 8, jnp.where(turn == 2, 20, 30))), before, mark, 0)
-        with jax.named_scope("wait_line"):
-            line_all(step, e).wait_recv()
-        with jax.named_scope("send_val"):
-            total = prod[step, 1, line, e]
-            for other in range(1, lines):
-                total = total + zrecv[step, lax.rem(line + other, lines), e]
-            for r in range(2):
-                for c in range(2):
-                    tout[turn, r * 4 : r * 4 + 4, c, :] = total[r, c * 4 : c * 4 + 4]
-
-            def send(n, carry):
-                r = lax.rem(cell // 8 + 1 + n // 4, 2)
-                m = lax.rem(n, 4)
-                x = lax.rem(cell + jnp.where(m == 0, 2, jnp.where(m == 1, 1, jnp.where(m == 2, 3, 0))), 4)
-                to = (r * 8 + lax.rem(side + step, 2) * 4 + x) * 2 + lax.rem(side + e, 2)
-                i = r * 4 + x
-
-                @pl.when(to != me)
-                def _():
-                    val_copy(step, turn, i, (1 - e) * band + e * mirror, to).start()
-
-                @pl.when(to == me)
-                def _():
-                    land[side, cell] = tout[turn, i]
-
-                return carry
-
-            lax.fori_loop(0, 8, send, 0)
-        return carry
-
-    lax.fori_loop(0, 4, second_half, 0)
-    with jax.named_scope("pair_pot"):
-        pot_all(1).wait_recv()
-        pot_all(2).wait_recv()
-        pot_pair().start()
 
     early = lax.rem(me // 8, 2)
     mine_first = early == side
@@ -406,8 +365,54 @@
         acc[...] += high + low
         return carry
 
+    def second_half(turn, carry):
+        step, e = turn // 2, 1 - lax.rem(turn, 2)
+        with jax.named_scope("mark1"):
+            before = jnp.where(turn == 0, 8, jnp.where(turn == 1, 20, jnp.where(turn == 2, 30, groups)))
+            lax.fori_loop(jnp.where(turn == 0, 8, jnp.where(turn == 1, 8, jnp.where(turn == 2, 20, 30))), before, mark, 0)
+        @pl.when(turn == 3)
+        def _():
+            with jax.named_scope("collect0"):
+                lax.fori_loop(0, 1, collect, 0)
+
+        with jax.named_scope("wait_line"):
+            line_all(step, e).wait_recv()
+        with jax.named_scope("send_val"):
+            total = prod[step, 1, line, e]
+            for other in range(1, lines):
+                total = total + zrecv[step, lax.rem(line + other, lines), e]
+            for r in range(2):
+                for c in range(2):
+                    tout[turn, r * 4 : r * 4 + 4, c, :] = total[r, c * 4 : c * 4 + 4]
+
+            def send(n, carry):
+                r = lax.rem(cell // 8 + 1 + n // 4, 2)
+                m = lax.rem(n, 4)
+                x = lax.rem(cell + jnp.where(m == 0, 2, jnp.where(m == 1, 1, jnp.where(m == 2, 3, 0))), 4)
+                to = (r * 8 + lax.rem(side + step, 2) * 4 + x) * 2 + lax.rem(side + e, 2)
+                i = r * 4 + x
+
+                @pl.when(to != me)
+                def _():
+                    val_copy(step, turn, i, (1 - e) * band + e * mirror, to).start()
+
+                @pl.when(to == me)
+                def _():
+                    land[side, cell] = tout[turn, i]
+
+                return carry
+
+            lax.fori_loop(0, 8, send, 0)
+        return carry
+
+    lax.fori_loop(0, 4, second_half, 0)
+    with jax.named_scope("pair_pot"):
+        pot_all(1).wait_recv()
+        pot_all(2).wait_recv()
+        pot_pair().start()
+
     with jax.named_scope("collect"):
-        lax.fori_loop(0, 8, collect, 0)
+        lax.fori_loop(1, 8, collect, 0)
     grid_field = acc[...]
 
     def pot_ready():

time: 44.1 us -> 43.6 us (0.989)
  no operation moved by 1% of the time
where the time goes in v6:
time: 43.6 us; the launch traced here: 43.5 us
  Pallas kernels  41.8 us (96%)
  local copies, waits for them, and re-layouts  1.67 us (4%)
    pallas_call x1, Pallas kernels, run(): pl.pallas_call(functools.partial(whole_kernel, box, window, radix), out_s...  41.8 us
    unnamed x1, local copies, waits for them, and re-layouts  1.67 us

profile of v6, /device:TPU:1, one launch (start us, length us, event | category | flops | bytes accessed | tf_op | source)
XLA Modules:
  0.0 43.5 jit_solution(2162624704361610503)
XLA Ops:
  0.0 41.8 %shard_map.91 = f32[1,2,32,1024]{3,2,1,0:T(8,128)} custom-call(f32[256,2,512]{2,1,0:T(2,128)} %coef_hbm.1, f32[1,16,256]{2,1,0:T(8,128)} %bitcast.5, f32[64,128]{1,0:T(8,128)} %pot_hbm.1, s32[1,16384]{1,0:T(1,128)} %bitcast.4, s32[32]{0:T(128)} %cnt_hbm.1, bf16[2,2,128,512]{3,2,1,0:T(8,128)(2,1)} %constant.8.clone.right_hbm, ...), custom_call_target="tpu_custom_call" | custom-call | tf_op jit(solution)/shard_map/pallas_call | solution.py:464
  41.8 1.7 %copy.11 = f32[1,2,32,1024]{3,2,1,0:T(8,128)} copy(f32[1,2,32,1024]{3,2,1,0:T(8,128)} %shard_map.91) | data formatting | bytes 524288

commit v7 on v6

--- a/solution.py
+++ b/solution.py
@@ -93,7 +93,7 @@
 def whole_kernel(
     box, window, radix, coef_hbm, rot_hbm, pot_hbm, idx_hbm, cnt_hbm, right_hbm, left_hbm, back_hbm, twist_hbm,
     out_ref, coef, coef_parts, rot_raw, rot_own, rots, prod, drecv, zrecv, tout, land, onehot, hits, acc, idx, cnt,
-    pot_out, right_tab, left_tab, back_tab, twist, right_blk, field, mixed, unmixed, turned, kinetic, out_buf,
+    pot_out, right_tab, left_tab, back_tab, twist, right_blk, mixed, unmixed, kinetic, out_buf,
     load_sem, rot_send, rot_recv, pot_send, pot_recv, pair_send, pair_recv, line_send, line_recv, val_send, val_recv,
     out_sem
 ):
@@ -327,8 +327,7 @@
     mine_first = early == side
     acc[...] = jnp.zeros_like(acc)
 
-    def collect(step, carry):
-        batch, near = step // 4, lax.rem(step, 4)
+    def row_part(batch, near):
         parity = lax.rem(early + batch, 2)
         row = lax.rem(cell // 4 + near + near // 2 - 2 * (near // 3), 4)
         alone = (parity == side) & (row == cell // 4)
@@ -341,8 +340,10 @@
         def _():
             val_all(0, batch, row, 4).wait_recv()
 
+        return parity, row
+
+    def row_sum(parity, row):
         deep = 4 * slots
-        span = pl.ds(pl.multiple_of(row * deep, deep), deep)
         cols = hits.shape[1]
         placed = [[], []]
         for u in range(4):
@@ -355,14 +356,23 @@
                     line_of = jnp.broadcast_to(part[c : c + 1, :], (16, slots)).astype(BF16)
                     pieces.append(mask * jnp.concatenate([line_of] * (cols // 16), axis=0))
                 placed[n].append(jnp.concatenate(pieces, axis=0))
-        picked = onehot[parity, :, span]
+        picked = onehot[parity, :, pl.ds(pl.multiple_of(row * deep, deep), deep)]
         high, low = (
             lax.dot_general(
                 picked, jnp.concatenate(part, axis=1), (((1,), (1,)), ((), ())), preferred_element_type=F32
             )
             for part in placed
         )
-        acc[...] += high + low
+        return high + low
+
+    def collect_pair(pair, carry):
+        batch, near = pair // 2, 2 * lax.rem(pair, 2)
+        first, second = row_part(batch, near), row_part(batch, near + 1)
+        acc[...] += row_sum(*first) + row_sum(*second)
+        return carry
+
+    def collect(step, carry):
+        acc[...] += row_sum(*row_part(step // 4, lax.rem(step, 4)))
         return carry
 
     def second_half(turn, carry):
@@ -373,7 +383,7 @@
         @pl.when(turn == 3)
         def _():
             with jax.named_scope("collect0"):
-                lax.fori_loop(0, 1, collect, 0)
+                collect(0, 0)
 
         with jax.named_scope("wait_line"):
             line_all(step, e).wait_recv()
@@ -412,7 +422,8 @@
         pot_pair().start()
 
     with jax.named_scope("collect"):
-        lax.fori_loop(1, 8, collect, 0)
+        lax.fori_loop(1, 4, collect, 0)
+        lax.fori_loop(2, 4, collect_pair, 0)
     grid_field = acc[...]
 
     def pot_ready():
@@ -423,7 +434,7 @@
 
     apply_kernel(
         box, window, radix, band >= 0, pot_ready, grid_field, pot_out, right_blk, left_tab, back_tab, twist,
-        field, mixed, unmixed, turned, kinetic, out_buf, lambda c: out_copy(c).start()
+        mixed, unmixed, kinetic, out_buf, lambda c: out_copy(c).start()
     )
     with jax.named_scope("wait_sends"):
         for c in range(2):
@@ -485,10 +496,8 @@
             pltpu.VMEM((groups,) + potential.shape, F32),
             *[pltpu.VMEM(table.shape, table.dtype) for table in consts],
             pltpu.VMEM((2, 2 * wide, 2 * radix * box), BF16),
-            pltpu.VMEM((rows, 2 * radix * box), F32),
             pltpu.VMEM((2, radix, 2 * window, radix * box), BF16),
             pltpu.VMEM((radix, 2 * window, radix * box), F32),
-            pltpu.VMEM((2, rows, 2 * radix * box), BF16),
             pltpu.VMEM((rows, wide), F32),
             pltpu.VMEM((2, window, window * window), F32),
             dma((10,)),
@@ -523,7 +532,7 @@
 
 def apply_kernel(
     box, window, radix, apart, pot_ready, grid_field, pot_ref, right_ref, left_ref, back_ref, twist_ref,
-    field_ref, mixed_ref, unmixed_ref, turned_ref, kinetic_ref, out_ref, ship
+    mixed_ref, unmixed_ref, kinetic_ref, out_ref, ship
 ):
     coarse = window // radix
     rows = radix * window
@@ -532,27 +541,33 @@
     lanes = 128
     per = wide // pot_ref.shape[2]
 
-    with jax.named_scope("fwd_right"):
-        field_ref[...] = dot3(split_parts(grid_field), [right_ref[0], right_ref[1]])
-
-    def mix(tile, carry):
-        at = pl.ds(pl.multiple_of(tile * lanes, lanes), lanes)
-        imag_at = pl.ds(pl.multiple_of(wide + tile * lanes, lanes), lanes)
-        values = []
-        for low in range(radix):
-            real = field_ref[low * window : (low + 1) * window, at]
-            imag = field_ref[low * window : (low + 1) * window, imag_at]
-            cos, sin = twist_ref[0, low : low + 1, at], twist_ref[1, low : low + 1, at]
-            values.append((real * cos - imag * sin, real * sin + imag * cos))
-        for k, pair in enumerate(fft8(values, 1)):
-            for c in range(2):
-                high, low = split_parts(pair[c])
-                mixed_ref[0, k, c * window : (c + 1) * window, at] = high
-                mixed_ref[1, k, c * window : (c + 1) * window, at] = low
-        return carry
-
-    with jax.named_scope("mix"):
-        lax.fori_loop(0, wide // lanes, mix, 0)
+    def columns(tile):
+        return slice(tile * lanes, (tile + 1) * lanes), slice(wide + tile * lanes, wide + (tile + 1) * lanes)
+
+    def right_of(tile):
+        return [jnp.concatenate([right_ref[i, :, at] for at in columns(tile)], axis=1) for i in range(2)]
+
+    def twist_of(low, at):
+        return twist_ref[0, low : low + 1, at], twist_ref[1, low : low + 1, at]
+
+    with jax.named_scope("fwd_mix"):
+        parts = split_parts(grid_field)
+        for tile in range(wide // lanes):
+            at = columns(tile)[0]
+            both = dot3(parts, right_of(tile))
+            values = []
+            for low in range(radix):
+                real = both[low * window : (low + 1) * window, :lanes]
+                imag = both[low * window : (low + 1) * window, lanes:]
+                if low:
+                    cos, sin = twist_of(low, at)
+                    real, imag = real * cos - imag * sin, real * sin + imag * cos
+                values.append((real, imag))
+            for k, pair in enumerate(fft8(values, 1)):
+                for c in range(2):
+                    high, low = split_parts(pair[c])
+                    mixed_ref[0, k, c * window : (c + 1) * window, at] = high
+                    mixed_ref[1, k, c * window : (c + 1) * window, at] = low
     with jax.named_scope("wait_pot"):
         pot_ready()
 
@@ -571,24 +586,24 @@
                     both = jnp.dot(back_ref[...], jnp.concatenate([high, low], axis=0), preferred_element_type=F32)
                     unmixed_ref[k, :, at] = both[: 2 * window] + both[2 * window :]
 
-    def unmix(tile, carry):
-        at = pl.ds(pl.multiple_of(tile * lanes, lanes), lanes)
-        imag_at = pl.ds(pl.multiple_of(wide + tile * lanes, lanes), lanes)
-        values = [
-            (unmixed_ref[k, :window, at], unmixed_ref[k, window:, at]) for k in range(radix)
-        ]
+    def unmix(tile):
+        at = columns(tile)[0]
+        values = [(unmixed_ref[k, :window, at], unmixed_ref[k, window:, at]) for k in range(radix)]
+        halves = [[], []]
         for low, (real, imag) in enumerate(fft8(values, -1)):
-            cos, sin = twist_ref[0, low : low + 1, at], twist_ref[1, low : low + 1, at]
-            turned = (real * cos + imag * sin, imag * cos - real * sin)
-            for value, to in zip(turned, (at, imag_at)):
-                for i, part in enumerate(split_parts(value)):
-                    turned_ref[i, low * window : (low + 1) * window, to] = part
-        return carry
-
-    with jax.named_scope("unmix"):
-        lax.fori_loop(0, wide // lanes, unmix, 0)
-    with jax.named_scope("back_right"):
-        applied = dot3([turned_ref[0], turned_ref[1]], [right_ref[0], right_ref[1]], ((1,), (1,)))
+            if low:
+                cos, sin = twist_of(low, at)
+                real, imag = real * cos + imag * sin, imag * cos - real * sin
+            split = [split_parts(real), split_parts(imag)]
+            for i in range(2):
+                halves[i].append(jnp.concatenate([split[0][i], split[1][i]], axis=1))
+        turned = [jnp.concatenate(half, axis=0) for half in halves]
+        return dot3(turned, right_of(tile), ((1,), (1,)))
+
+    with jax.named_scope("unmix_back"):
+        applied = unmix(0)
+        for tile in range(1, wide // lanes):
+            applied = applied + unmix(tile)
 
     kinetic = kinetic_ref[...]
     applied = applied + jnp.concatenate([kinetic, kinetic], axis=1) * grid_field

time: 43.6 us -> 42.6 us (0.977)
  Pallas kernels: 41.8 us -> 40.8 us
    pallas_call x1, Pallas kernels: 41.8 us -> 40.8 us  [run(): pl.pallas_call(functools.partial(whole_kernel, box, window, radix), out_s...]
where the time goes in v7:
time: 42.6 us; the launch traced here: 42.5 us
  Pallas kernels  40.8 us (96%)
  local copies, waits for them, and re-layouts  1.67 us (4%)
    pallas_call x1, Pallas kernels, run(): pl.pallas_call(functools.partial(whole_kernel, box, window, radix), out_s...  40.8 us
    unnamed x1, local copies, waits for them, and re-layouts  1.67 us

profile of v7, /device:TPU:1, one launch (start us, length us, event | category | flops | bytes accessed | tf_op | source)
XLA Modules:
  0.0 42.5 jit_solution(13138741271714706654)
XLA Ops:
  0.0 40.8 %shard_map.91 = f32[1,2,32,1024]{3,2,1,0:T(8,128)} custom-call(f32[256,2,512]{2,1,0:T(2,128)} %coef_hbm.1, f32[1,16,256]{2,1,0:T(8,128)} %bitcast.5, f32[64,128]{1,0:T(8,128)} %pot_hbm.1, s32[1,16384]{1,0:T(1,128)} %bitcast.4, s32[32]{0:T(128)} %cnt_hbm.1, bf16[2,2,128,512]{3,2,1,0:T(8,128)(2,1)} %constant.8.clone.right_hbm, ...), custom_call_target="tpu_custom_call" | custom-call | tf_op jit(solution)/shard_map/pallas_call | solution.py:475
  40.8 1.7 %copy.11 = f32[1,2,32,1024]{3,2,1,0:T(8,128)} copy(f32[1,2,32,1024]{3,2,1,0:T(8,128)} %shard_map.91) | data formatting | bytes 524288

commit v8 on v7

--- a/solution.py
+++ b/solution.py
@@ -133,9 +133,8 @@
         lax.fori_loop(0, 7, body, jnp.int32(0xC431FD7))
 
     def lines_other(act):
-        low = 1 - line // 2
         for step in range(lines):
-            l = low * (lines - 1 - step) + (1 - low) * step
+            l = side * (lines - 1 - step) + (1 - side) * step
 
             @pl.when(l != line)
             def _(l=l):
@@ -304,7 +303,7 @@
         with jax.named_scope("pair"):
             pair_copy(step).wait_recv()
             prod[step, 1] = prod[step, 1] + drecv[step]
-            for e in (1, 0):
+            for e in (side, 1 - side):
                 lines_other(lambda l: line_copy(step, e, l).start())
 
         @pl.when(step == 1)
@@ -376,14 +375,14 @@
         return carry
 
     def second_half(turn, carry):
-        step, e = turn // 2, 1 - lax.rem(turn, 2)
+        step, e = turn // 2, lax.rem(side + turn, 2)
         with jax.named_scope("mark1"):
             before = jnp.where(turn == 0, 8, jnp.where(turn == 1, 20, jnp.where(turn == 2, 30, groups)))
             lax.fori_loop(jnp.where(turn == 0, 8, jnp.where(turn == 1, 8, jnp.where(turn == 2, 20, 30))), before, mark, 0)
         @pl.when(turn == 3)
         def _():
             with jax.named_scope("collect0"):
-                collect(0, 0)
+                lax.fori_loop(0, 2 - side, collect, 0)
 
         with jax.named_scope("wait_line"):
             line_all(step, e).wait_recv()
@@ -422,7 +421,7 @@
         pot_pair().start()
 
     with jax.named_scope("collect"):
-        lax.fori_loop(1, 4, collect, 0)
+        lax.fori_loop(2 - side, 4, collect, 0)
         lax.fori_loop(2, 4, collect_pair, 0)
     grid_field = acc[...]
 

time: 42.6 us -> 42.6 us (level)
  no operation moved by 1% of the time
where the time goes in v8:
time: 42.6 us; the launch traced here: 42.5 us
  Pallas kernels  40.8 us (96%)
  local copies, waits for them, and re-layouts  1.67 us (4%)
    pallas_call x1, Pallas kernels, run(): pl.pallas_call(functools.partial(whole_kernel, box, window, radix), out_s...  40.8 us
    unnamed x1, local copies, waits for them, and re-layouts  1.67 us

profile of v8, /device:TPU:1, one launch (start us, length us, event | category | flops | bytes accessed | tf_op | source)
XLA Modules:
  0.0 42.5 jit_solution(17360399037702279125)
XLA Ops:
  0.0 40.8 %shard_map.91 = f32[1,2,32,1024]{3,2,1,0:T(8,128)} custom-call(f32[256,2,512]{2,1,0:T(2,128)} %coef_hbm.1, f32[1,16,256]{2,1,0:T(8,128)} %bitcast.5, f32[64,128]{1,0:T(8,128)} %pot_hbm.1, s32[1,16384]{1,0:T(1,128)} %bitcast.4, s32[32]{0:T(128)} %cnt_hbm.1, bf16[2,2,128,512]{3,2,1,0:T(8,128)(2,1)} %constant.8.clone.right_hbm, ...), custom_call_target="tpu_custom_call" | custom-call | tf_op jit(solution)/shard_map/pallas_call | solution.py:474
  40.8 1.7 %copy.11 = f32[1,2,32,1024]{3,2,1,0:T(8,128)} copy(f32[1,2,32,1024]{3,2,1,0:T(8,128)} %shard_map.91) | data formatting | bytes 524288

commit v9 on v8

--- a/solution.py
+++ b/solution.py
@@ -197,13 +197,13 @@
         part = pot_out.at[me, share]
         return remote(part, part, pot_send.at[0], pot_recv.at[0], mirror, across)
 
-    def pot_copy(which, piece, q):
-        part = pot_out.at[piece, share]
-        return remote(part, part, pot_send.at[which], pot_recv.at[which], band, q * 2 + side)
-
-    def pot_all(which):
-        part = pot_out.at[pl.ds(0, plane - 1), pl.ds(0, half_rows)]
-        return remote(part, part, pot_send.at[which], pot_recv.at[which], band, across)
+    def pot_copy(q):
+        part = pot_out.at[pl.ds(2 * cell, 2), share]
+        return remote(part, part, pot_send.at[1], pot_recv.at[1], band, q * 2 + side)
+
+    def pot_all():
+        part = pot_out.at[pl.ds(0, 2 * (plane - 1)), pl.ds(0, half_rows)]
+        return remote(part, part, pot_send.at[1], pot_recv.at[1], band, across)
 
     def pot_pair():
         part = pot_out.at[:, share]
@@ -309,8 +309,7 @@
         @pl.when(step == 1)
         def _():
             with jax.named_scope("relay_pot"):
-                peers(lambda q: pot_copy(1, me, q).start())
-                peers(lambda q: pot_copy(2, across, q).start())
+                peers(lambda q: pot_copy(q).start())
 
         return carry
 
@@ -416,8 +415,7 @@
 
     lax.fori_loop(0, 4, second_half, 0)
     with jax.named_scope("pair_pot"):
-        pot_all(1).wait_recv()
-        pot_all(2).wait_recv()
+        pot_all().wait_recv()
         pot_pair().start()
 
     with jax.named_scope("collect"):
@@ -442,8 +440,7 @@
         rot_all(1).wait_send()
         rot_all(2).wait_send()
         pot_swap().wait_send()
-        pot_all(1).wait_send()
-        pot_all(2).wait_send()
+        pot_all().wait_send()
         pot_pair().wait_send()
         for step in range(2):
             pair_copy(step).wait_send()

time: 42.6 us -> 42.6 us (level)
  no operation moved by 1% of the time
where the time goes in v9:
time: 42.6 us; the launch traced here: 42.5 us
  Pallas kernels  40.8 us (96%)
  local copies, waits for them, and re-layouts  1.67 us (4%)
    pallas_call x1, Pallas kernels, run(): pl.pallas_call(functools.partial(whole_kernel, box, window, radix), out_s...  40.8 us
    unnamed x1, local copies, waits for them, and re-layouts  1.67 us

profile of v9, /device:TPU:1, one launch (start us, length us, event | category | flops | bytes accessed | tf_op | source)
XLA Modules:
  0.0 42.5 jit_solution(15888492031110314979)
XLA Ops:
  0.0 40.8 %shard_map.91 = f32[1,2,32,1024]{3,2,1,0:T(8,128)} custom-call(f32[256,2,512]{2,1,0:T(2,128)} %coef_hbm.1, f32[1,16,256]{2,1,0:T(8,128)} %bitcast.5, f32[64,128]{1,0:T(8,128)} %pot_hbm.1, s32[1,16384]{1,0:T(1,128)} %bitcast.4, s32[32]{0:T(128)} %cnt_hbm.1, bf16[2,2,128,512]{3,2,1,0:T(8,128)(2,1)} %constant.8.clone.right_hbm, ...), custom_call_target="tpu_custom_call" | custom-call | tf_op jit(solution)/shard_map/pallas_call | solution.py:471
  40.8 1.7 %copy.11 = f32[1,2,32,1024]{3,2,1,0:T(8,128)} copy(f32[1,2,32,1024]{3,2,1,0:T(8,128)} %shard_map.91) | data formatting | bytes 524288

commit v10 on v9

--- a/solution.py
+++ b/solution.py
@@ -302,8 +302,8 @@
 
         with jax.named_scope("pair"):
             pair_copy(step).wait_recv()
-            prod[step, 1] = prod[step, 1] + drecv[step]
             for e in (side, 1 - side):
+                prod[step, 1, :, e] = prod[step, 1, :, e] + drecv[step, :, e]
                 lines_other(lambda l: line_copy(step, e, l).start())
 
         @pl.when(step == 1)
@@ -420,7 +420,8 @@
 
     with jax.named_scope("collect"):
         lax.fori_loop(2 - side, 4, collect, 0)
-        lax.fori_loop(2, 4, collect_pair, 0)
+        lax.fori_loop(2, 3, collect_pair, 0)
+        lax.fori_loop(6, 8, collect, 0)
     grid_field = acc[...]
 
     def pot_ready():

time: 42.6 us -> 42.8 us (level)
  no operation moved by 1% of the time
where the time goes in v10:
time: 42.8 us; the launch traced here: 42.7 us
  Pallas kernels  41 us (96%)
  local copies, waits for them, and re-layouts  1.67 us (4%)
    pallas_call x1, Pallas kernels, run(): pl.pallas_call(functools.partial(whole_kernel, box, window, radix), out_s...  41 us
    unnamed x1, local copies, waits for them, and re-layouts  1.67 us

profile of v10, /device:TPU:1, one launch (start us, length us, event | category | flops | bytes accessed | tf_op | source)
XLA Modules:
  0.0 42.7 jit_solution(14893118649875021178)
XLA Ops:
  0.0 41.0 %shard_map.91 = f32[1,2,32,1024]{3,2,1,0:T(8,128)} custom-call(f32[256,2,512]{2,1,0:T(2,128)} %coef_hbm.1, f32[1,16,256]{2,1,0:T(8,128)} %bitcast.5, f32[64,128]{1,0:T(8,128)} %pot_hbm.1, s32[1,16384]{1,0:T(1,128)} %bitcast.4, s32[32]{0:T(128)} %cnt_hbm.1, bf16[2,2,128,512]{3,2,1,0:T(8,128)(2,1)} %constant.8.clone.right_hbm, ...), custom_call_target="tpu_custom_call" | custom-call | tf_op jit(solution)/shard_map/pallas_call | solution.py:472
  41.0 1.7 %copy.11 = f32[1,2,32,1024]{3,2,1,0:T(8,128)} copy(f32[1,2,32,1024]{3,2,1,0:T(8,128)} %shard_map.91) | data formatting | bytes 524288

commit v11 on v9

--- a/solution.py
+++ b/solution.py
@@ -381,7 +381,7 @@
         @pl.when(turn == 3)
         def _():
             with jax.named_scope("collect0"):
-                lax.fori_loop(0, 2 - side, collect, 0)
+                lax.fori_loop(0, 3 - 2 * side, collect, 0)
 
         with jax.named_scope("wait_line"):
             line_all(step, e).wait_recv()
@@ -419,7 +419,7 @@
         pot_pair().start()
 
     with jax.named_scope("collect"):
-        lax.fori_loop(2 - side, 4, collect, 0)
+        lax.fori_loop(3 - 2 * side, 4, collect, 0)
         lax.fori_loop(2, 4, collect_pair, 0)
     grid_field = acc[...]
 

time: 42.6 us -> 42.6 us (level)
  no operation moved by 1% of the time
where the time goes in v11:
time: 42.6 us; the launch traced here: 42.5 us
  Pallas kernels  40.8 us (96%)
  local copies, waits for them, and re-layouts  1.67 us (4%)
    pallas_call x1, Pallas kernels, run(): pl.pallas_call(functools.partial(whole_kernel, box, window, radix), out_s...  40.8 us
    unnamed x1, local copies, waits for them, and re-layouts  1.67 us

profile of v11, /device:TPU:1, one launch (start us, length us, event | category | flops | bytes accessed | tf_op | source)
XLA Modules:
  0.0 42.5 jit_solution(8507754003593516671)
XLA Ops:
  0.0 40.8 %shard_map.91 = f32[1,2,32,1024]{3,2,1,0:T(8,128)} custom-call(f32[256,2,512]{2,1,0:T(2,128)} %coef_hbm.1, f32[1,16,256]{2,1,0:T(8,128)} %bitcast.5, f32[64,128]{1,0:T(8,128)} %pot_hbm.1, s32[1,16384]{1,0:T(1,128)} %bitcast.4, s32[32]{0:T(128)} %cnt_hbm.1, bf16[2,2,128,512]{3,2,1,0:T(8,128)(2,1)} %constant.8.clone.right_hbm, ...), custom_call_target="tpu_custom_call" | custom-call | tf_op jit(solution)/shard_map/pallas_call | solution.py:471
  40.8 1.7 %copy.11 = f32[1,2,32,1024]{3,2,1,0:T(8,128)} copy(f32[1,2,32,1024]{3,2,1,0:T(8,128)} %shard_map.91) | data formatting | bytes 524288
